TPU v7x, 32 devices: a 4x4x1 block of a 4x4x8 slice. The times are simulated.
32 devices in a mesh: dp: 1 (over z), tp: 4 (over y), sp: 8 (over x, core).
Axes of the slice: x: 4, y: 4, z: 1, core: 2. Of those that a mesh axis runs over, the one named last changes fastest.
The devices are a block of a 4x4x8 slice.
Arguments:
- x: bfloat16 [4096, 3584], P(('dp', 'sp'))
- pos: int32 [4096], P(('dp', 'sp'))
- k_hist: bfloat16 [2, 8192, 4, 128], P(None, ('dp', 'sp'), 'tp')
- v_hist: bfloat16 [2, 8192, 4, 128], P(None, ('dp', 'sp'), 'tp')
- wq: bfloat16 [2, 3584, 3584], P(None, None, 'tp')
- wk: bfloat16 [2, 3584, 512], P(None, None, 'tp')
- wv: bfloat16 [2, 3584, 512], P(None, None, 'tp')
- wo: bfloat16 [2, 3584, 3584], P(None, 'tp')
- wg: bfloat16 [2, 3584, 18944], P(None, None, 'tp')
- wu: bfloat16 [2, 3584, 18944], P(None, None, 'tp')
- wd: bfloat16 [2, 18944, 3584], P(None, 'tp')
- g1: bfloat16 [2, 3584], replicated
- g2: bfloat16 [2, 3584], replicated
Outputs:
- output 1: bfloat16 [4096, 3584], P(('dp', 'sp'))
- output 2: bfloat16 [2, 4096, 4, 128], P(None, ('dp', 'sp'), 'tp')
- output 3: bfloat16 [2, 4096, 4, 128], P(None, ('dp', 'sp'), 'tp')
All inputs are finite; a program needn't handle non-finite values.
Results may differ from a plain program's by a relative error of at most 0.02.
Values are sent between devices in bfloat16 or wider.
A program may use at most 768 MiB of HBM per device.

v0:
```python
import jax
import jax.numpy as jnp
from jax import lax
from jax.sharding import PartitionSpec as P

EPS = 1e-5
ROPE_THETA = 500000.0
QB = 64


def rmsnorm(x, g):
    xf = x.astype(jnp.float32)
    r = lax.rsqrt(jnp.mean(xf * xf, axis=-1, keepdims=True) + EPS)
    return (xf * r * g.astype(jnp.float32)).astype(jnp.bfloat16)


def rope(t, pos):
    half = t.shape[-1] // 2
    inv = ROPE_THETA ** (-(jnp.arange(half, dtype=jnp.float32) * (2.0 / t.shape[-1])))
    ang = pos.astype(jnp.float32)[..., None] * inv
    c = jnp.cos(ang)[..., None, :]
    s = jnp.sin(ang)[..., None, :]
    tf = t.astype(jnp.float32)
    t1 = tf[..., :half]
    t2 = tf[..., half:]
    return jnp.concatenate([t1 * c - t2 * s, t2 * c + t1 * s], axis=-1).astype(jnp.bfloat16)


def mm(a, b):
    return jnp.dot(a, b, preferred_element_type=jnp.float32)


def partial_attn(qq, k, v, mask=None):
    s = jnp.einsum('qkgd,tkd->qkgt', qq, k, preferred_element_type=jnp.float32) * (k.shape[-1] ** -0.5)
    if mask is not None:
        s = jnp.where(mask, s, -jnp.inf)
    m = jnp.max(s, axis=-1)
    p = jnp.exp(s - m[..., None])
    o = jnp.einsum('qkgt,tkd->qkgd', p.astype(jnp.bfloat16), v, preferred_element_type=jnp.float32)
    return m, jnp.sum(p, axis=-1), o


def solution(mesh):
    sp = mesh.shape['sp']
    row = ('dp', 'sp')
    kv_spec = P(None, row, 'tp', None)
    col = P(None, None, 'tp')
    rowsplit = P(None, 'tp', None)

    def body(x, pos, k_hist, v_hist, wq, wk, wv, wo, wg, wu, wd, g1, g2):
        n, d = x.shape
        layers, _, kvl, dh = k_hist.shape
        hql = wq.shape[-1] // dh
        g = hql // kvl
        s_tot = n * sp
        idx = lax.axis_index('sp')
        kpos = jnp.arange(s_tot)
        starts = idx * n + jnp.arange(n // QB) * QB
        ks, vs = [], []
        for l in range(layers):
            h = rmsnorm(x, g1[l])
            q = rope(mm(h, wq[l]).astype(jnp.bfloat16).reshape(n, hql, dh), pos)
            k = rope(mm(h, wk[l]).astype(jnp.bfloat16).reshape(n, kvl, dh), pos)
            v = mm(h, wv[l]).astype(jnp.bfloat16).reshape(n, kvl, dh)
            ks.append(k)
            vs.append(v)

            q_all = lax.all_gather(q, 'sp', axis=0, tiled=True).reshape(s_tot // QB, QB, kvl, g, dh)
            kh = k_hist[l]
            vh = v_hist[l]
            m_h, l_h, o_h = lax.map(lambda qq: partial_attn(qq, kh, vh), q_all)
            m_h = m_h.reshape(s_tot, kvl, g)
            m_g = lax.pmax(m_h, 'sp')
            sc = jnp.exp(m_h - m_g)
            o_h = lax.psum_scatter(o_h.reshape(s_tot, kvl, g, dh) * sc[..., None], 'sp', scatter_dimension=0, tiled=True)
            l_h = lax.psum_scatter(l_h.reshape(s_tot, kvl, g) * sc, 'sp', scatter_dimension=0, tiled=True)
            m_h = lax.dynamic_slice_in_dim(m_g, idx * n, n, axis=0)

            k_all = lax.all_gather(k, 'sp', axis=0, tiled=True)
            v_all = lax.all_gather(v, 'sp', axis=0, tiled=True)

            def new_blk(args, k_all=k_all, v_all=v_all):
                st, qq = args
                mask = (kpos[None, :] <= (st + jnp.arange(QB))[:, None])[:, None, None, :]
                return partial_attn(qq, k_all, v_all, mask)

            m_n, l_n, o_n = lax.map(new_blk, (starts, q.reshape(n // QB, QB, kvl, g, dh)))
            m_n = m_n.reshape(n, kvl, g)
            l_n = l_n.reshape(n, kvl, g)
            o_n = o_n.reshape(n, kvl, g, dh)
            mt = jnp.maximum(m_h, m_n)
            a_h = jnp.exp(m_h - mt)
            a_n = jnp.exp(m_n - mt)
            den = l_h * a_h + l_n * a_n
            o = (o_h * a_h[..., None] + o_n * a_n[..., None]) / den[..., None]
            attn = o.astype(jnp.bfloat16).reshape(n, hql * dh)
            x = x + lax.psum(mm(attn, wo[l]), 'tp').astype(jnp.bfloat16)

            h2 = rmsnorm(x, g2[l])
            a = mm(h2, wg[l]).astype(jnp.bfloat16)
            b = mm(h2, wu[l]).astype(jnp.bfloat16)
            u = (jax.nn.silu(a.astype(jnp.float32)) * b.astype(jnp.float32)).astype(jnp.bfloat16)
            x = x + lax.psum(mm(u, wd[l]), 'tp').astype(jnp.bfloat16)
        return x, jnp.stack(ks), jnp.stack(vs)

    in_specs = (P(row, None), P(row), kv_spec, kv_spec, col, col, col, rowsplit, col, col, rowsplit, P(), P())
    out_specs = (P(row, None), kv_spec, kv_spec)
    return jax.shard_map(body, mesh=mesh, in_specs=in_specs, out_specs=out_specs, check_vma=False)
```

profile of v0, /device:TPU:100, one launch (start us, length us, event | category | flops | bytes accessed | tf_op | source)
XLA Modules:
  0.0 1739.8 jit_solution(1786443641144015803)
XLA Ops:
  30.9 39.1 %all-gather.9.cloned.1.call-done = bf16[4096,7,128]{0,2,1:T(8,128)(2,1)} async-done(((bf16[512,7,128]{0,2,1:T(8,128)(2,1)}), bf16[4096,7,128]{0,2,1:T(8,128)(2,1)}) %all-gather.9.cloned.1.call-update) | async-done | bytes 7340048 | tf_op jit(solution)/shard_map/all_gather | solution.py:68
  87.9 203.6 %while.58 = (s32[]{:T(128)}, f32[64,64,1,7]{1,0,2,3:T(8,128)S(1)}, f32[64,64,1,7]{1,0,2,3:T(8,128)S(1)}, f32[64,64,1,7,128]{4,1,0,3,2:T(8,128)}, bf16[64,64,1,7,...) while((s32[]{:T(128)}, f32[64,64,1,7]{1,0,2,3:T(8,128)S(1)}, ...), condition=%wide.region_4.5_spmd, body=%wide.region_1.4_spmd.sunk | while | flops 238550144 | bytes 6396005 | solution.py:71
  298.1 45.0 %all-reduce.7.cloned.1.call-done = f32[4096,1,7]{0,1,2:T(1,128)} async-done(((f32[4096,1,7]{0,1,2:T(1,128)}), f32[4096,1,7]{0,1,2:T(1,128)}) %all-reduce.7.cloned.1.call-update) | async-done | bytes 114704 | tf_op jit(solution)/shard_map/pmax | solution.py:73
  353.1 11.0 bitcast_reduce_fusion.3
  364.2 11.6 bitcast_multiply_fusion.1
  391.6 49.2 %while.60 = (s32[]{:T(128)}, f32[8,64,1,7]{1,0,2,3:T(8,128)S(1)}, f32[8,64,1,7]{1,0,2,3:T(8,128)S(1)}, f32[8,64,1,7,128]{4,1,0,3,2:T(8,128)}, s32[8]{0:T(128)S(1...) while((s32[]{:T(128)}, f32[8,64,1,7]{1,0,2,3:T(8,128)S(1)}, ...), condition=%wide.region_10.11_spmd.clone, body=%wide.region_7.10_spmd.clone.sunk | while | flops 952630464 | bytes 29202588 | solution.py:87
  444.1 60.1 %reduce-scatter.9.cloned.1.call-done = f32[512,1,7,128]{3,0,2,1:T(8,128)} async-done(((f32[4096,1,7,128]{3,0,2,1:T(8,128)}), f32[512,1,7,128]{3,0,2,1:T(8,128)}) %reduce-scatter.9.cloned.1.call-update) | async-done | bytes 1835024 | tf_op jit(solution)/shard_map/reduce_scatter | solution.py:75
  517.4 133.9 %all-reduce.10 = bf16[512,3584]{1,0:T(8,128)(2,1)} all-reduce(f32[512,3584]{1,0:T(8,128)} %fusion.124), channel_id=1, replica_groups=mesh['dp'=1,'tp'=4,'sp'=8] {'tp'}, use_global_device_ids=true, to_apply=%region_12.13 | all-reduce | flops 1835008 | bytes 11010048 | tf_op jit(solution)/shard_map/psum | solution.py:97
  657.9 26.3 %fusion.96 = bf16[512,4736]{1,0:T(8,128)(2,1)} fusion(bf16[2,3584,4736]{2,1,0:T(8,128)(2,1)} %param.29, bf16[512,3584]{1,0:T(8,128)(2,1)S(1)} %get-tuple-element.400, f32[3584]{0:T(1024)S(1)} %get-tuple-element.327, f32[512]{0:T(512)S(1)} %add_rsqrt_fusion.2), kind=kOutput, calls=%fused_computation.116 | convolution fusion | flops 17390960640 | bytes 42483712 | tf_op jit(solution)/shard_map/dot_general | solution.py:30
  684.1 28.2 %fusion.248 = bf16[512,4736]{1,0:T(8,128)(2,1)} fusion(bf16[512,4736]{1,0:T(8,128)(2,1)} %fusion.96, bf16[2,3584,4736]{2,1,0:T(8,128)(2,1)} %param.30, bf16[512,3584]{1,0:T(8,128)(2,1)} %copy-done.3, f32[3584]{0:T(1024)S(1)} %get-tuple-element.327, f32[512]{0:T(512)S(1)} %add_rsqrt_fusion.2), kind=kOutput, calls=%fused_computation.107.clone.clone.2 | convolution fusion | flops 17410359296 | bytes 47333376 | tf_op jit(solution)/shard_map/dot_general | solution.py:30
  712.4 27.2 %fusion.74 = f32[512,3584]{1,0:T(8,128)} fusion(bf16[2,4736,3584]{2,1,0:T(8,128)(2,1)} %param.31, bf16[512,4736]{1,0:T(8,128)(2,1)} %fusion.248), kind=kOutput, calls=%fused_computation.78 | convolution fusion | flops 17381195776 | bytes 46137344 | tf_op jit(solution)/shard_map/dot_general | solution.py:30
  739.6 129.0 %all-reduce.11 = bf16[512,3584]{1,0:T(8,128)(2,1)} all-reduce(f32[512,3584]{1,0:T(8,128)} %fusion.74), channel_id=1, replica_groups=mesh['dp'=1,'tp'=4,'sp'=8] {'tp'}, use_global_device_ids=true, to_apply=%region_14.15 | all-reduce | flops 1835008 | bytes 11010048 | tf_op jit(solution)/shard_map/psum | solution.py:103
  891.3 37.4 %all-gather.13.cloned.1.call-done = bf16[4096,7,128]{0,2,1:T(8,128)(2,1)} async-done(((bf16[512,7,128]{0,2,1:T(8,128)(2,1)}), bf16[4096,7,128]{0,2,1:T(8,128)(2,1)}) %all-gather.13.cloned.1.call-update) | async-done | bytes 7340048 | tf_op jit(solution)/shard_map/all_gather | solution.py:68
  946.6 203.6 %while.59 = (s32[]{:T(128)}, f32[64,64,1,7]{1,0,2,3:T(8,128)S(1)}, f32[64,64,1,7]{1,0,2,3:T(8,128)S(1)}, f32[64,64,1,7,128]{4,1,0,3,2:T(8,128)}, bf16[64,64,1,7,...) while((s32[]{:T(128)}, f32[64,64,1,7]{1,0,2,3:T(8,128)S(1)}, ...), condition=%wide.region_19.20_spmd, body=%wide.region_16.19_spmd.sunk | while | flops 238550144 | bytes 6396005 | solution.py:71
  1156.4 45.4 %all-reduce.9.cloned.1.call-done = f32[4096,1,7]{0,1,2:T(1,128)} async-done(((f32[4096,1,7]{0,1,2:T(1,128)}), f32[4096,1,7]{0,1,2:T(1,128)}) %all-reduce.9.cloned.1.call-update) | async-done | bytes 114704 | tf_op jit(solution)/shard_map/pmax | solution.py:73
  1211.8 11.0 bitcast_reduce_fusion.2
  1223.1 11.6 bitcast_multiply_fusion
  1250.3 47.5 %while.61 = (s32[]{:T(128)}, f32[8,64,1,7]{1,0,2,3:T(8,128)S(1)}, f32[8,64,1,7]{1,0,2,3:T(8,128)S(1)}, f32[8,64,1,7,128]{4,1,0,3,2:T(8,128)}, s32[8]{0:T(128)S(1...) while((s32[]{:T(128)}, f32[8,64,1,7]{1,0,2,3:T(8,128)S(1)}, ...), condition=%wide.region_25.26_spmd.clone, body=%wide.region_22.25_spmd.clone.sunk | while | flops 952630464 | bytes 29202588 | solution.py:87
  1301.1 61.4 %reduce-scatter.11.cloned.1.call-done = f32[512,1,7,128]{3,0,2,1:T(8,128)} async-done(((f32[4096,1,7,128]{3,0,2,1:T(8,128)}), f32[512,1,7,128]{3,0,2,1:T(8,128)}) %reduce-scatter.11.cloned.1.call-update) | async-done | bytes 1835024 | tf_op jit(solution)/shard_map/reduce_scatter | solution.py:75
  1375.6 133.9 %all-reduce.12 = bf16[512,3584]{1,0:T(8,128)(2,1)} all-reduce(f32[512,3584]{1,0:T(8,128)} %fusion.120), channel_id=1, replica_groups=mesh['dp'=1,'tp'=4,'sp'=8] {'tp'}, use_global_device_ids=true, to_apply=%region_27.28 | all-reduce | flops 1835008 | bytes 11010048 | tf_op jit(solution)/shard_map/psum | solution.py:97
  1516.1 26.2 %fusion.102 = bf16[512,4736]{1,0:T(8,128)(2,1)} fusion(bf16[2,3584,4736]{2,1,0:T(8,128)(2,1)} %param.29, bf16[512,3584]{1,0:T(8,128)(2,1)S(1)} %get-tuple-element.391, f32[3584]{0:T(1024)S(1)} %copy-done.25, f32[512]{0:T(512)S(1)} %add_rsqrt_fusion), kind=kOutput, calls=%fused_computation.118 | convolution fusion | flops 17390960640 | bytes 42483712 | tf_op jit(solution)/shard_map/dot_general | solution.py:30
  1542.3 28.1 %fusion.244 = bf16[512,4736]{1,0:T(8,128)(2,1)} fusion(bf16[512,4736]{1,0:T(8,128)(2,1)} %fusion.102, bf16[2,3584,4736]{2,1,0:T(8,128)(2,1)} %param.30, bf16[512,3584]{1,0:T(8,128)(2,1)} %copy-done.4, f32[3584]{0:T(1024)S(1)} %copy-done.25, f32[512]{0:T(512)S(1)} %add_rsqrt_fusion), kind=kOutput, calls=%fused_computation.106.clone.clone.2 | convolution fusion | flops 17410359296 | bytes 47333376 | tf_op jit(solution)/shard_map/dot_general | solution.py:30
  1570.5 27.3 %fusion.68 = f32[512,3584]{1,0:T(8,128)} fusion(bf16[2,4736,3584]{2,1,0:T(8,128)(2,1)} %param.31, bf16[512,4736]{1,0:T(8,128)(2,1)} %fusion.244), kind=kOutput, calls=%fused_computation.72 | convolution fusion | flops 17381195776 | bytes 46137344 | tf_op jit(solution)/shard_map/dot_general | solution.py:30
  1597.8 128.9 %all-reduce.13 = bf16[512,3584]{1,0:T(8,128)(2,1)} all-reduce(f32[512,3584]{1,0:T(8,128)} %fusion.68), channel_id=1, replica_groups=mesh['dp'=1,'tp'=4,'sp'=8] {'tp'}, use_global_device_ids=true, to_apply=%region_29.30 | all-reduce | flops 1835008 | bytes 11010048 | tf_op jit(solution)/shard_map/psum | solution.py:103
  (1265 shorter events, 693.2 us)
Async XLA Ops:
  7.2 62.8 %all-gather.9.cloned.1.call-start = ((), (), s32[]{:S(2)}) async-start(), calls=%async_computation.4 | async-start | bytes 8257536 | tf_op jit(solution)/shard_map/all_gather | solution.py:68
  7.3 22.1 %copy-start.26 = (f32[64]{0:T(128)}, f32[64]{0:T(128)S(1)}, u32[]{:S(2)}) copy-start(f32[64]{0:T(128)S(1)} %negate_power_fusion) | copy-start | bytes 772
  8.0 21.5 %copy-start.22 = (f32[512]{0:T(512)}, f32[512]{0:T(512)S(1)}, u32[]{:S(2)}) copy-start(f32[512]{0:T(512)S(1)} %convert_element_type.193) | copy-start | bytes 6148
  25.6 317.6 %all-reduce.7.cloned.1.call-start = ((), (), s32[]{:S(2)}) async-start(), calls=%async_computation.5 | async-start | bytes 229376 | tf_op jit(solution)/shard_map/pmax | solution.py:73
  30.0 262.5 %copy-start.13 = (bf16[512,1,64]{0,2,1:T(8,128)(2,1)}, bf16[512,1,64]{0,2,1:T(8,128)(2,1)S(1)}, u32[]{:S(2)}) copy-start(bf16[512,1,64]{0,2,1:T(8,128)(2,1)S(1)} %get-tuple-element.424) | copy-start | bytes 196612
  30.0 262.5 %copy-start.15 = (bf16[512,1,64]{0,2,1:T(8,128)(2,1)}, bf16[512,1,64]{0,2,1:T(8,128)(2,1)S(1)}, u32[]{:S(2)}) copy-start(bf16[512,1,64]{0,2,1:T(8,128)(2,1)S(1)} %get-tuple-element.425) | copy-start | bytes 196612
  292.4 89.6 %all-gather.11.cloned.1.call-start = ((), (), s32[]{:S(2)}) async-start(), calls=%async_computation.7 | async-start | bytes 1179648 | tf_op jit(solution)/shard_map/all_gather | solution.py:79
  293.2 49.9 %copy-start.11 = (f32[4096,1,7]{0,1,2:T(1,128)S(1)}, f32[4096,1,7]{0,1,2:T(1,128)}, u32[]{:S(2)}) copy-start(f32[4096,1,7]{0,1,2:T(1,128)} %reshape.615) | copy-start | bytes 344068
  293.2 96.9 %all-gather.17.cloned.1.call-start = ((), (), s32[]{:S(2)}) async-start(), calls=%async_computation.12 | async-start | bytes 1179648 | tf_op jit(solution)/shard_map/all_gather | solution.py:80
  297.5 143.6 %reduce-scatter.13.cloned.1.call-start = ((), (), s32[]{:S(2)}) async-start(), calls=%async_computation.14 | async-start | bytes 2359296
  364.1 140.1 %reduce-scatter.9.cloned.1.call-start = ((), (), s32[]{:S(2)}) async-start(), calls=%async_computation.6 | async-start | bytes 16515072 | tf_op jit(solution)/shard_map/reduce_scatter | solution.py:75
  375.9 552.8 %all-gather.13.cloned.1.call-start = ((), (), s32[]{:S(2)}) async-start(), calls=%async_computation.8 | async-start | bytes 8257536 | tf_op jit(solution)/shard_map/all_gather | solution.py:68
  440.9 76.5 %copy-start.28 = (s32[8]{0:T(128)}, s32[8]{0:T(128)S(1)}, u32[]{:S(2)}) copy-start(s32[8]{0:T(128)S(1)} %get-tuple-element.792) | copy-start | bytes 100
  875.1 9.9 copy-start.8
  875.1 9.9 copy-start.10
  886.5 315.3 %all-reduce.9.cloned.1.call-start = ((), (), s32[]{:S(2)}) async-start(), calls=%async_computation.9 | async-start | bytes 229376 | tf_op jit(solution)/shard_map/pmax | solution.py:73
  939.5 7.1 copy-start.5
  939.5 7.1 copy-start.6
  1151.1 90.6 %all-gather.15.cloned.1.call-start = ((), (), s32[]{:S(2)}) async-start(), calls=%async_computation.11 | async-start | bytes 1179648 | tf_op jit(solution)/shard_map/all_gather | solution.py:79
  1151.9 49.9 %copy-start.12 = (f32[4096,1,7]{0,1,2:T(1,128)S(1)}, f32[4096,1,7]{0,1,2:T(1,128)}, u32[]{:S(2)}) copy-start(f32[4096,1,7]{0,1,2:T(1,128)} %reshape.624) | copy-start | bytes 344068
  1151.9 96.9 %all-gather.19.cloned.1.call-start = ((), (), s32[]{:S(2)}) async-start(), calls=%async_computation.13 | async-start | bytes 1179648 | tf_op jit(solution)/shard_map/all_gather | solution.py:80
  1156.2 141.9 %reduce-scatter.15.cloned.1.call-start = ((), (), s32[]{:S(2)}) async-start(), calls=%async_computation.15 | async-start | bytes 2359296
  1222.8 139.6 %reduce-scatter.11.cloned.1.call-start = ((), (), s32[]{:S(2)}) async-start(), calls=%async_computation.10 | async-start | bytes 16515072 | tf_op jit(solution)/shard_map/reduce_scatter | solution.py:75
  1236.1 14.2 copy-start.29
  (32 other events, 111.5 us)
Sparse Core Ops, SparseCore 0:
  25.7 44.2 all-gather.8
  292.5 50.5 all-reduce.6
  344.7 23.4 all-gather.10
  369.7 20.3 all-gather.16
  392.9 27.6 reduce-scatter.12
  422.8 81.4 reduce-scatter.8
  886.6 42.0 all-gather.12
  1151.2 50.5 all-reduce.8
  1203.4 23.4 all-gather.14
  1228.4 20.3 all-gather.18
  1251.2 27.6 reduce-scatter.14
  1281.1 81.3 reduce-scatter.10
where the time goes:
time: 1750 us; the launch traced here: 1740 us
  matrix products  593 us (34%)
  blocking collectives  526 us (30%)
  waiting for transfers between devices  301 us (17%)
  other arithmetic  160 us (9%)
  local copies, waits for them, and re-layouts  135 us (8%)
    psum x2, blocking collectives, body(): x = x + lax.psum(mm(attn, wo[l]), 'tp').astype(jnp.bfloat16)  268 us
    psum x2, blocking collectives, body(): x = x + lax.psum(mm(u, wd[l]), 'tp').astype(jnp.bfloat16)  258 us
    dot_general x14, matrix products, mm(): return jnp.dot(a, b, preferred_element_type=jnp.float32)  214 us
    dot_general x144, matrix products, partial_attn(): jnp.einsum('qkgd,tkd->qkgt', qq, k, preferred_element_type=jnp.float32)  200 us
    dot_general x144, matrix products, partial_attn(): jnp.einsum('qkgt,tkd->qkgd', p.astype(jnp.bfloat16), v, preferred_element...  179 us
    reduce_scatter x2, waiting for transfers between devices, body(): lax.psum_scatter(o_h.reshape(s_tot, kvl, g, dh) * sc[..., None], 'sp', sc...  122 us
    pmax x2, waiting for transfers between devices, body(): m_g = lax.pmax(m_h, 'sp')  90.5 us
    reduce_sum x144, other arithmetic, partial_attn(): return (m, jnp.sum(p, axis=-1), o)  76.5 us
  transfers between devices with their start and end apart: 12, of which 8 were waited for; matrix products, arithmetic and copies ran while one was open for 12% of the time, Pallas kernels for 0%

commit v1 on v0

v1 whole, which is shorter than its diff:
```python
import functools

import jax
import jax.numpy as jnp
from jax import lax
from jax.experimental import pallas as pl
from jax.experimental.pallas import tpu as pltpu
from jax.sharding import PartitionSpec as P

EPS = 1e-5
ROPE_THETA = 500000.0
LOG2E = 1.4426950408889634


def rmsnorm(x, g):
    xf = x.astype(jnp.float32)
    r = lax.rsqrt(jnp.mean(xf * xf, axis=-1, keepdims=True) + EPS)
    return (xf * r * g.astype(jnp.float32)).astype(jnp.bfloat16)


def rope(t, pos):
    half = t.shape[-1] // 2
    inv = ROPE_THETA ** (-(jnp.arange(half, dtype=jnp.float32) * (2.0 / t.shape[-1])))
    ang = pos.astype(jnp.float32)[..., None] * inv
    c = jnp.cos(ang)[..., None, :]
    s = jnp.sin(ang)[..., None, :]
    tf = t.astype(jnp.float32)
    t1 = tf[..., :half]
    t2 = tf[..., half:]
    return jnp.concatenate([t1 * c - t2 * s, t2 * c + t1 * s], axis=-1).astype(jnp.bfloat16)


def mm(a, b):
    return jnp.dot(a, b, preferred_element_type=jnp.float32)


def attn_kernel(sp, layer, q_ref, hist_ref, new_ref, o_ref, hkv, nkv, m_ref, l_ref, acc_ref, hsem, nsem):
    n, w = q_ref.shape
    dh = hkv.shape[-1]
    heads = w // dh
    hc = hkv.shape[2]
    nc = nkv.shape[2]
    rows_t = min(256, n)
    nt = n // rows_t
    c = dh ** -0.5 * LOG2E
    me = lax.axis_index("sp")
    for b in range(sp):
        for j in range(2):
            pltpu.make_async_copy(hist_ref.at[b, 2 * layer + j], hkv.at[b, j], hsem.at[b, j]).start()
    for b in range(sp):
        pltpu.make_async_copy(new_ref.at[b], nkv.at[b], nsem.at[b]).start()
    m_ref[...] = jnp.full(m_ref.shape, -1e30, jnp.float32)
    l_ref[...] = jnp.zeros_like(l_ref)
    acc_ref[...] = jnp.zeros_like(acc_ref)

    def block(t, k_of, v_of, cols, mask):
        rows = pl.ds(pl.multiple_of(t * rows_t, rows_t), rows_t)

        def qk(g):
            return lax.dot_general(q_ref[rows, g * dh:(g + 1) * dh], k_of(), (((1,), (1,)), ((), ())),
                                   preferred_element_type=jnp.float32)

        s = qk(0)
        pend = None

        def pv(g, p, alpha):
            acc_ref[g, rows, :] = acc_ref[g, rows, :] * alpha + mm(p, v_of())

        for g in range(heads):
            s_next = qk(g + 1) if g + 1 < heads else None
            if pend is not None:
                pv(*pend)
            if mask is not None:
                s = jnp.where(mask, s, -jnp.inf)
            m_old = m_ref[g, rows, :]
            m_new = jnp.maximum(m_old, jnp.max(s, axis=1, keepdims=True) * c)
            alpha = jnp.exp2(m_old - m_new)
            p = jnp.exp2(s * c - m_new[:, :1])
            ls = p[:, :dh]
            for j in range(1, cols // dh):
                ls = ls + p[:, j * dh:(j + 1) * dh]
            l_ref[g, rows, :] = l_ref[g, rows, :] * alpha + ls
            m_ref[g, rows, :] = m_new
            pend = (g, p.astype(jnp.bfloat16), alpha)
            s = s_next
        pv(*pend)

    def hist_body(i, carry):
        b = i // nt
        t = i % nt

        @pl.when(t == 0)
        def _():
            for j in range(2):
                pltpu.make_async_copy(hist_ref.at[b, 2 * layer + j], hkv.at[b, j], hsem.at[b, j]).wait()

        block(t, lambda: hkv[b, 0], lambda: hkv[b, 1], hc, None)
        return carry

    lax.fori_loop(0, sp * nt, hist_body, 0)
    for b in range(sp):
        pltpu.make_async_copy(new_ref.at[b], nkv.at[b], nsem.at[b]).wait()

    def new_body(i, carry):
        b = i // nt
        block(i % nt, lambda: nkv[b, 0], lambda: nkv[b, 1], nc, None)
        return carry

    lax.fori_loop(0, me * nt, new_body, 0)

    def diag_body(t, carry):
        r = lax.broadcasted_iota(jnp.int32, (rows_t, nc), 0) + t * rows_t
        col = lax.broadcasted_iota(jnp.int32, (rows_t, nc), 1)
        block(t, lambda: nkv[me, 0], lambda: nkv[me, 1], nc, col <= r)
        return carry

    lax.fori_loop(0, nt, diag_body, 0)
    for g in range(heads):
        l = jnp.sum(l_ref[g], axis=1, keepdims=True)
        o_ref[:, g * dh:(g + 1) * dh] = (acc_ref[g] / l).astype(jnp.bfloat16)


def attention(sp, layer, q, hist, new):
    n, w = q.shape
    _, _, hc, dh = hist.shape
    heads = w // dh
    keys = sp * hc + sp * n // 2
    return pl.pallas_call(
        functools.partial(attn_kernel, sp, layer),
        out_shape=jax.ShapeDtypeStruct((n, w), jnp.bfloat16),
        in_specs=[pl.BlockSpec(memory_space=pltpu.VMEM), pl.BlockSpec(memory_space=pl.ANY),
                  pl.BlockSpec(memory_space=pl.ANY)],
        out_specs=pl.BlockSpec(memory_space=pltpu.VMEM),
        scratch_shapes=[
            pltpu.VMEM((sp, 2, hc, dh), jnp.bfloat16),
            pltpu.VMEM((sp, 2, n, dh), jnp.bfloat16),
            pltpu.VMEM((heads, n, dh), jnp.float32),
            pltpu.VMEM((heads, n, dh), jnp.float32),
            pltpu.VMEM((heads, n, dh), jnp.float32),
            pltpu.SemaphoreType.DMA((sp, 2)),
            pltpu.SemaphoreType.DMA((sp,)),
        ],
        compiler_params=pltpu.CompilerParams(vmem_limit_bytes=40 * 2 ** 20),
        cost_estimate=pl.CostEstimate(flops=4 * n * w * keys, bytes_accessed=4 * keys * dh, transcendentals=n * heads * keys),
        name="attention",
    )(q, hist, new)


def solution(mesh):
    sp = mesh.shape['sp']
    tp = mesh.shape['tp']
    row = ('dp', 'sp')
    kv_spec = P(None, row, 'tp', None)
    col = P(None, None, 'tp')
    rowsplit = P(None, 'tp', None)

    def body(x, pos, k_hist, v_hist, wq, wk, wv, wo, wg, wu, wd, g1, g2):
        n, d = x.shape
        layers, hc, kvl, dh = k_hist.shape
        hql = wq.shape[-1] // dh
        dt = d // tp
        my = lax.axis_index('tp') * dt
        kv = jnp.stack([k_hist[:, :, 0], v_hist[:, :, 0]], axis=1).reshape(2 * layers, hc, dh)
        hist = lax.all_gather(kv, 'sp', axis=0)
        ks, vs = [], []

        def reduce_add(x, part):
            red = lax.psum_scatter(part, 'tp', scatter_dimension=1, tiled=True)
            xc = lax.dynamic_slice_in_dim(x, my, dt, axis=1) + red.astype(jnp.bfloat16)
            return lax.all_gather(xc, 'tp', axis=1, tiled=True)

        for l in range(layers):
            h = rmsnorm(x, g1[l])
            k = rope(mm(h, wk[l]).astype(jnp.bfloat16).reshape(n, kvl, dh), pos)
            v = mm(h, wv[l]).astype(jnp.bfloat16).reshape(n, kvl, dh)
            ks.append(k)
            vs.append(v)
            new = lax.all_gather(jnp.stack([k[:, 0], v[:, 0]]), 'sp', axis=0)
            q = rope(mm(h, wq[l]).astype(jnp.bfloat16).reshape(n, hql, dh), pos)
            attn = attention(sp, l, q.reshape(n, hql * dh), hist, new)
            x = reduce_add(x, mm(attn, wo[l]))
            h2 = rmsnorm(x, g2[l])
            a = mm(h2, wg[l]).astype(jnp.bfloat16)
            b = mm(h2, wu[l]).astype(jnp.bfloat16)
            u = (jax.nn.silu(a.astype(jnp.float32)) * b.astype(jnp.float32)).astype(jnp.bfloat16)
            x = reduce_add(x, mm(u, wd[l]))
        return x, jnp.stack(ks), jnp.stack(vs)

    in_specs = (P(row, None), P(row), kv_spec, kv_spec, col, col, col, rowsplit, col, col, rowsplit, P(), P())
    out_specs = (P(row, None), kv_spec, kv_spec)
    return jax.shard_map(body, mesh=mesh, in_specs=in_specs, out_specs=out_specs, check_vma=False)
```

time: 1750 us -> 954 us (0.55)
  blocking collectives: 526 us -> 0 us
  matrix products: 593 us -> 212 us
  waiting for transfers between devices: 301 us -> 536 us
  Pallas kernels: 0 us -> 132 us
  other arithmetic: 160 us -> 28.7 us
  local copies, waits for them, and re-layouts: 135 us -> 25.1 us
    psum x4 -> x0, blocking collectives: 526 us -> none  [the longest x2 268 us: body(): x = x + lax.psum(mm(attn, wo[l]), 'tp').astype(jnp.bfloat16)]
    dot_general x288 -> x0, matrix products: 379 us -> none  [the longest x144 200 us: partial_attn(): jnp.einsum('qkgd,tkd->qkgt', qq, k, preferred_element_type=jnp.float32)]
    reduce_scatter x2 -> x4, waiting for transfers between devices: 122 us -> 305 us  [reduce_add(): red = lax.psum_scatter(part, 'tp', scatter_dimension=1, tiled=True)]
    all_gather x6 -> x7, waiting for transfers between devices: 88.5 us -> 230 us  [the longest x4 161 us: reduce_add(): return lax.all_gather(xc, 'tp', axis=1, tiled=True)]
    pallas_call x0 -> x2, Pallas kernels: none -> 132 us  [attention(): pl.pallas_call(functools.partial(attn_kernel, sp, layer), out_shape=jax.S...]
    pmax x2 -> x0, waiting for transfers between devices: 90.5 us -> none  [body(): m_g = lax.pmax(m_h, 'sp')]
    reduce_sum x144 -> x0, other arithmetic: 76.5 us -> none  [partial_attn(): return (m, jnp.sum(p, axis=-1), o)]
    unnamed x77 -> x71, local copies, waits for them, and re-layouts: 57.9 us -> 17.4 us
  transfers between devices with their start and end apart: 12 -> 11, of which waited for: 8 -> 11; matrix products, arithmetic and copies ran while one was open for 12% -> 3% of each run, Pallas kernels for 0% -> 0%
where the time goes in v1:
time: 954 us; the launch traced here: 949 us
  waiting for transfers between devices  536 us (56%)
  matrix products  212 us (22%)
  Pallas kernels  132 us (14%)
  other arithmetic  28.7 us (3%)
  local copies, waits for them, and re-layouts  25.1 us (3%)
  between operations  14.6 us (2%)
    reduce_scatter x4, waiting for transfers between devices, reduce_add(): red = lax.psum_scatter(part, 'tp', scatter_dimension=1, tiled=True)  305 us
    dot_general x14, matrix products, mm(): return jnp.dot(a, b, preferred_element_type=jnp.float32)  212 us
    all_gather x4, waiting for transfers between devices, reduce_add(): return lax.all_gather(xc, 'tp', axis=1, tiled=True)  161 us
    pallas_call x2, Pallas kernels, attention(): pl.pallas_call(functools.partial(attn_kernel, sp, layer), out_shape=jax.S...  132 us
    all_gather x1, waiting for transfers between devices, body(): hist = lax.all_gather(kv, 'sp', axis=0)  49 us
    all_gather x2, waiting for transfers between devices, body(): new = lax.all_gather(jnp.stack([k[:, 0], v[:, 0]]), 'sp', axis=0)  20.1 us
  transfers between devices with their start and end apart: 11, of which 11 were waited for; matrix products, arithmetic and copies ran while one was open for 3% of the time, Pallas kernels for 0%

profile of v1, /device:TPU:100, one launch (start us, length us, event | category | flops | bytes accessed | tf_op | source)
XLA Modules:
  0.0 949.0 jit_solution(15989433921258889507)
XLA Ops:
  22.0 9.2 fusion.79
  34.8 10.2 %all-gather.20.cloned.1.call-done = bf16[16,512,128]{2,1,0:T(8,128)(2,1)} async-done(((bf16[2,512,128]{2,1,0:T(8,128)(2,1)}), bf16[16,512,128]{2,1,0:T(8,128)(2,1)}) %all-gather.20.cloned.1.call-update) | async-done | bytes 2097168 | tf_op jit(solution)/shard_map/all_gather | solution.py:178
  45.0 49.0 %all-gather.10.cloned.1.call-done.hist_ref = bf16[8,4,1024,128]{3,2,1,0:T(8,128)(2,1)} async-done(((bf16[1,4,1024,128]{3,2,1,0:T(8,128)(2,1)}), bf16[8,4,1024,128]{3,2,1,0:T(8,128)(2,1)}) %all-gather.10.cloned.1.call-update) | async-done | bytes 8388624 | tf_op jit(solution)/shard_map/all_gather | solution.py:164
  99.0 66.1 %attention.2 = bf16[512,896]{1,0:T(8,128)(2,1)S(1)} custom-call(bf16[512,896]{1,0:T(8,128)(2,1)S(1)} %copy.38.q_ref, bf16[8,4,1024,128]{3,2,1,0:T(8,128)(2,1)S(1)} %copy-done, bf16[8,2,512,128]{3,2,1,0:T(8,128)(2,1)S(1)} %bitcast.115), custom_call_target="tpu_custom_call" | custom-call | flops 18790481920 | bytes 5242880 | tf_op jit(solution)/shard_map/attention/pallas_call | solution.py:128
  165.1 8.8 fusion.56
  174.0 82.1 %reduce-scatter.5.cloned.1.call-done = f32[512,896]{1,0:T(8,128)} async-done(((f32[512,3584]{1,0:T(8,128)}), f32[512,896]{1,0:T(8,128)}) %reduce-scatter.5.cloned.1.call-update) | async-done | bytes 1835024 | tf_op jit(solution)/shard_map/reduce_scatter | solution.py:168
  259.7 40.2 %all-gather.12.cloned.1.call-done = bf16[512,3584]{1,0:T(8,128)(2,1)} async-done(((bf16[512,896]{1,0:T(8,128)(2,1)}), bf16[512,3584]{1,0:T(8,128)(2,1)}) %all-gather.12.cloned.1.call-update) | async-done | bytes 3670032 | tf_op jit(solution)/shard_map/all_gather | solution.py:170
  302.8 27.3 %fusion.28 = bf16[512,4736]{1,0:T(8,128)(2,1)} fusion(bf16[2,3584,4736]{2,1,0:T(8,128)(2,1)} %param.21, bf16[512,3584]{1,0:T(8,128)(2,1)} %all-gather.12.cloned.1.call-done, f32[3584]{0:T(1024)S(1)} %get-tuple-element.13, f32[512]{0:T(512)S(1)} %add_rsqrt_fusion.2), kind=kOutput, calls=%fused_computation.40 | convolution fusion | flops 17390960640 | bytes 42483712 | tf_op jit(solution)/shard_map/dot_general | solution.py:34
  330.1 27.9 %fusion.162 = bf16[512,4736]{1,0:T(8,128)(2,1)} fusion(bf16[512,4736]{1,0:T(8,128)(2,1)} %fusion.28, bf16[2,3584,4736]{2,1,0:T(8,128)(2,1)} %param.22, bf16[512,3584]{1,0:T(8,128)(2,1)} %all-gather.12.cloned.1.call-done, f32[3584]{0:T(1024)S(1)} %get-tuple-element.13, f32[512]{0:T(512)S(1)} %add_rsqrt_fusion.2), kind=kOutput, calls=%fused_computation.31.clone.clone.2 | convolution fusion | flops 17410359296 | bytes 47333376 | tf_op jit(solution)/shard_map/dot_general | solution.py:34
  358.0 27.4 %fusion.6 = f32[512,3584]{1,0:T(8,128)} fusion(bf16[2,4736,3584]{2,1,0:T(8,128)(2,1)} %param.23, bf16[512,4736]{1,0:T(8,128)(2,1)} %fusion.162), kind=kOutput, calls=%fused_computation.6 | convolution fusion | flops 17381195776 | bytes 46137344 | tf_op jit(solution)/shard_map/dot_general | solution.py:34
  385.5 70.4 %reduce-scatter.7.cloned.1.call-done = f32[512,896]{1,0:T(8,128)} async-done(((f32[512,3584]{1,0:T(8,128)}), f32[512,896]{1,0:T(8,128)}) %reduce-scatter.7.cloned.1.call-update) | async-done | bytes 1835024 | tf_op jit(solution)/shard_map/reduce_scatter | solution.py:168
  458.9 40.9 %all-gather.14.cloned.1.call-done = bf16[512,3584]{1,0:T(8,128)(2,1)} async-done(((bf16[512,896]{1,0:T(8,128)(2,1)}), bf16[512,3584]{1,0:T(8,128)(2,1)}) %all-gather.14.cloned.1.call-update) | async-done | bytes 3670032 | tf_op jit(solution)/shard_map/all_gather | solution.py:170
  510.1 9.2 fusion.85
  522.3 9.9 %all-gather.22.cloned.1.call-done = bf16[16,512,128]{2,1,0:T(8,128)(2,1)} async-done(((bf16[2,512,128]{2,1,0:T(8,128)(2,1)}), bf16[16,512,128]{2,1,0:T(8,128)(2,1)}) %all-gather.22.cloned.1.call-update) | async-done | bytes 2097168 | tf_op jit(solution)/shard_map/all_gather | solution.py:178
  537.1 65.6 %attention.3 = bf16[512,896]{1,0:T(8,128)(2,1)S(1)} custom-call(bf16[512,896]{1,0:T(8,128)(2,1)S(1)} %copy.42.q_ref, bf16[8,4,1024,128]{3,2,1,0:T(8,128)(2,1)S(1)} %copy-done.1, bf16[8,2,512,128]{3,2,1,0:T(8,128)(2,1)S(1)} %bitcast.116), custom_call_target="tpu_custom_call" | custom-call | flops 18790481920 | bytes 5242880 | tf_op jit(solution)/shard_map/attention/pallas_call | solution.py:128
  602.7 8.8 fusion.52
  611.6 82.5 %reduce-scatter.9.cloned.1.call-done = f32[512,896]{1,0:T(8,128)} async-done(((f32[512,3584]{1,0:T(8,128)}), f32[512,896]{1,0:T(8,128)}) %reduce-scatter.9.cloned.1.call-update) | async-done | bytes 1835024 | tf_op jit(solution)/shard_map/reduce_scatter | solution.py:168
  697.0 40.9 %all-gather.16.cloned.1.call-done = bf16[512,3584]{1,0:T(8,128)(2,1)} async-done(((bf16[512,896]{1,0:T(8,128)(2,1)}), bf16[512,3584]{1,0:T(8,128)(2,1)}) %all-gather.16.cloned.1.call-update) | async-done | bytes 3670032 | tf_op jit(solution)/shard_map/all_gather | solution.py:170
  740.7 27.7 %fusion.34 = bf16[512,4736]{1,0:T(8,128)(2,1)} fusion(bf16[2,3584,4736]{2,1,0:T(8,128)(2,1)} %param.21, bf16[512,3584]{1,0:T(8,128)(2,1)} %all-gather.16.cloned.1.call-done, f32[3584]{0:T(1024)S(1)} %copy-done.28, f32[512]{0:T(512)S(1)} %add_rsqrt_fusion), kind=kOutput, calls=%fused_computation.42 | convolution fusion | flops 17390960640 | bytes 42483712 | tf_op jit(solution)/shard_map/dot_general | solution.py:34
  768.5 28.0 %fusion.158 = bf16[512,4736]{1,0:T(8,128)(2,1)} fusion(bf16[512,4736]{1,0:T(8,128)(2,1)} %fusion.34, bf16[2,3584,4736]{2,1,0:T(8,128)(2,1)} %param.22, bf16[512,3584]{1,0:T(8,128)(2,1)} %all-gather.16.cloned.1.call-done, f32[3584]{0:T(1024)S(1)} %copy-done.28, f32[512]{0:T(512)S(1)} %add_rsqrt_fusion), kind=kOutput, calls=%fused_computation.30.clone.clone.2 | convolution fusion | flops 17410359296 | bytes 47333376 | tf_op jit(solution)/shard_map/dot_general | solution.py:34
  796.5 27.2 %fusion = f32[512,3584]{1,0:T(8,128)} fusion(bf16[2,4736,3584]{2,1,0:T(8,128)(2,1)} %param.23, bf16[512,4736]{1,0:T(8,128)(2,1)} %fusion.158), kind=kOutput, calls=%fused_computation | convolution fusion | flops 17381195776 | bytes 46137344 | tf_op jit(solution)/shard_map/dot_general | solution.py:34
  823.9 70.4 %reduce-scatter.11.cloned.1.call-done = f32[512,896]{1,0:T(8,128)} async-done(((f32[512,3584]{1,0:T(8,128)}), f32[512,896]{1,0:T(8,128)}) %reduce-scatter.11.cloned.1.call-update) | async-done | bytes 1835024 | tf_op jit(solution)/shard_map/reduce_scatter | solution.py:168
  899.0 39.2 %all-gather.18.cloned.1.call-done = bf16[512,3584]{1,0:T(8,128)(2,1)} async-done(((bf16[512,896]{1,0:T(8,128)(2,1)}), bf16[512,3584]{1,0:T(8,128)(2,1)}) %all-gather.18.cloned.1.call-update) | async-done | bytes 3670032 | tf_op jit(solution)/shard_map/all_gather | solution.py:170
  938.2 4.1 copy.48
  (131 shorter events, 61.5 us)
Async XLA Ops:
  7.2 37.9 %all-gather.20.cloned.1.call-start = ((), (), s32[]{:S(2)}) async-start(), calls=%async_computation.13 | async-start | bytes 2359296 | tf_op jit(solution)/shard_map/all_gather | solution.py:178
  7.3 25.7 %copy-start.29 = (f32[64]{0:T(128)}, f32[64]{0:T(128)S(1)}, u32[]{:S(2)}) copy-start(f32[64]{0:T(128)S(1)} %negate_power_fusion) | copy-start | bytes 772
  20.3 73.7 %all-gather.10.cloned.1.call-start = ((), (), s32[]{:S(2)}) async-start(), calls=%async_computation.4 | async-start | bytes 9437184 | tf_op jit(solution)/shard_map/all_gather | solution.py:164
  21.6 234.5 %reduce-scatter.5.cloned.1.call-start = ((), (), s32[]{:S(2)}) async-start(), calls=%async_computation.5 | async-start | bytes 9175040 | tf_op jit(solution)/shard_map/reduce_scatter | solution.py:168
  173.9 85.2 %copy-start.24 = (bf16[2,3584]{1,0:T(2,128)(2,1)S(1)}, bf16[2,3584]{1,0:T(2,128)(2,1)}, u32[]{:S(2)}) copy-start(bf16[2,3584]{1,0:T(2,128)(2,1)} %param.25) | copy-start | bytes 43012
  173.9 126.0 %all-gather.12.cloned.1.call-start = ((), (), s32[]{:S(2)}) async-start(), calls=%async_computation.6 | async-start | bytes 4587520 | tf_op jit(solution)/shard_map/all_gather | solution.py:170
  259.0 197.0 %reduce-scatter.7.cloned.1.call-start = ((), (), s32[]{:S(2)}) async-start(), calls=%async_computation.7 | async-start | bytes 9175040 | tf_op jit(solution)/shard_map/reduce_scatter | solution.py:168
  385.4 117.4 %copy-start.27 = (f32[3584]{0:T(1024)S(1)}, f32[3584]{0:T(1024)}, u32[]{:S(2)}) copy-start(f32[3584]{0:T(1024)} %get-tuple-element.14) | copy-start | bytes 43012
  385.4 117.4 %copy-start.32 = (bf16[2,3584,128]{2,1,0:T(8,128)(2,1)S(1)}, bf16[2,3584,128]{2,1,0:T(8,128)(2,1)}, u32[]{:S(2)}) copy-start(bf16[2,3584,128]{2,1,0:T(8,128)(2,1)} %param.18) | copy-start | bytes 5505028
  385.5 114.3 %all-gather.14.cloned.1.call-start = ((), (), s32[]{:S(2)}) async-start(), calls=%async_computation.8 | async-start | bytes 4587520 | tf_op jit(solution)/shard_map/all_gather | solution.py:170
  458.8 47.5 %copy-start.26 = (f32[512]{0:T(512)S(1)}, f32[512]{0:T(512)}, u32[]{:S(2)}) copy-start(f32[512]{0:T(512)} %copy-done.25) | copy-start | bytes 6148
  458.8 47.5 %copy-start.30 = (f32[64]{0:T(128)S(1)}, f32[64]{0:T(128)}, u32[]{:S(2)}) copy-start(f32[64]{0:T(128)} %copy-done.29) | copy-start | bytes 772
  458.9 73.3 %all-gather.22.cloned.1.call-start = ((), (), s32[]{:S(2)}) async-start(), calls=%async_computation.14 | async-start | bytes 2359296 | tf_op jit(solution)/shard_map/all_gather | solution.py:178
  510.0 184.1 %reduce-scatter.9.cloned.1.call-start = ((), (), s32[]{:S(2)}) async-start(), calls=%async_computation.9 | async-start | bytes 9175040 | tf_op jit(solution)/shard_map/reduce_scatter | solution.py:168
  611.5 129.2 %copy-start.28 = (f32[3584]{0:T(1024)S(1)}, f32[3584]{0:T(1024)}, u32[]{:S(2)}) copy-start(f32[3584]{0:T(1024)} %get-tuple-element.12) | copy-start | bytes 43012
  611.6 126.3 %all-gather.16.cloned.1.call-start = ((), (), s32[]{:S(2)}) async-start(), calls=%async_computation.10 | async-start | bytes 4587520 | tf_op jit(solution)/shard_map/all_gather | solution.py:170
  697.0 197.4 %reduce-scatter.11.cloned.1.call-start = ((), (), s32[]{:S(2)}) async-start(), calls=%async_computation.11 | async-start | bytes 9175040 | tf_op jit(solution)/shard_map/reduce_scatter | solution.py:168
  823.7 73.5 %copy-start.21 = (bf16[512,128]{0,1:T(8,128)(2,1)S(1)}, bf16[512,128]{0,1:T(8,128)(2,1)}, u32[]{:S(2)}) copy-start(bf16[512,128]{0,1:T(8,128)(2,1)} %copy-done.20) | copy-start | bytes 393220
  823.7 73.5 %copy-start.23 = (bf16[512,128]{0,1:T(8,128)(2,1)S(1)}, bf16[512,128]{0,1:T(8,128)(2,1)}, u32[]{:S(2)}) copy-start(bf16[512,128]{0,1:T(8,128)(2,1)} %copy-done.22) | copy-start | bytes 393220
  823.7 74.4 %copy-start.11 = (bf16[512,1,64]{0,2,1:T(8,128)(2,1)S(1)}, bf16[512,1,64]{0,2,1:T(8,128)(2,1)}, u32[]{:S(2)}) copy-start(bf16[512,1,64]{0,2,1:T(8,128)(2,1)} %copy-done.10) | copy-start | bytes 196612
  823.7 74.4 %copy-start.13 = (bf16[512,1,64]{0,2,1:T(8,128)(2,1)S(1)}, bf16[512,1,64]{0,2,1:T(8,128)(2,1)}, u32[]{:S(2)}) copy-start(bf16[512,1,64]{0,2,1:T(8,128)(2,1)} %copy-done.12) | copy-start | bytes 196612
  823.7 74.4 %copy-start.15 = (bf16[512,1,64]{0,2,1:T(8,128)(2,1)S(1)}, bf16[512,1,64]{0,2,1:T(8,128)(2,1)}, u32[]{:S(2)}) copy-start(bf16[512,1,64]{0,2,1:T(8,128)(2,1)} %copy-done.14) | copy-start | bytes 196612
  823.8 74.4 %copy-start.17 = (bf16[512,1,64]{0,2,1:T(8,128)(2,1)S(1)}, bf16[512,1,64]{0,2,1:T(8,128)(2,1)}, u32[]{:S(2)}) copy-start(bf16[512,1,64]{0,2,1:T(8,128)(2,1)} %copy-done.16) | copy-start | bytes 196612
  823.8 114.3 %all-gather.18.cloned.1.call-start = ((), (), s32[]{:S(2)}) async-start(), calls=%async_computation.12 | async-start | bytes 4587520 | tf_op jit(solution)/shard_map/all_gather | solution.py:170
  (21 other events, 106.2 us)
Sparse Core Ops, SparseCore 0:
  20.4 24.5 all-gather.19
  46.7 47.3 all-gather.9
  174.1 82.0 reduce-scatter.4
  259.1 40.7 all-gather.11
  385.6 70.3 reduce-scatter.6
  459.0 40.7 all-gather.13
  510.1 22.0 all-gather.21
  611.7 82.3 reduce-scatter.8
  697.1 40.7 all-gather.15
  823.9 70.3 reduce-scatter.10
  897.3 40.7 all-gather.17

commit v2 on v1

--- a/solution.py
+++ b/solution.py
@@ -128,8 +128,8 @@
     return pl.pallas_call(
         functools.partial(attn_kernel, sp, layer),
         out_shape=jax.ShapeDtypeStruct((n, w), jnp.bfloat16),
-        in_specs=[pl.BlockSpec(memory_space=pltpu.VMEM), pl.BlockSpec(memory_space=pl.ANY),
-                  pl.BlockSpec(memory_space=pl.ANY)],
+        in_specs=[pl.BlockSpec(memory_space=pltpu.VMEM), pl.BlockSpec(memory_space=pltpu.HBM),
+                  pl.BlockSpec(memory_space=pltpu.HBM)],
         out_specs=pl.BlockSpec(memory_space=pltpu.VMEM),
         scratch_shapes=[
             pltpu.VMEM((sp, 2, hc, dh), jnp.bfloat16),
@@ -140,10 +140,391 @@
             pltpu.SemaphoreType.DMA((sp, 2)),
             pltpu.SemaphoreType.DMA((sp,)),
         ],
-        compiler_params=pltpu.CompilerParams(vmem_limit_bytes=40 * 2 ** 20),
+        compiler_params=pltpu.CompilerParams(vmem_limit_bytes=60 * 2 ** 20),
         cost_estimate=pl.CostEstimate(flops=4 * n * w * keys, bytes_accessed=4 * keys * dh, transcendentals=n * heads * keys),
         name="attention",
     )(q, hist, new)
+
+
+MESH = pl.DeviceIdType.MESH
+LN = 128
+
+
+def mlp_kernel(T, layer, attn_ref, x_ref, wo_ref, g_ref, wg_ref, wu_ref, wd_ref, out_ref,
+               acc, ring, H, U, wdb, RA, RB, RD, RU, XF, xm, st, strv,
+               ags, agr, rss, rsr, sts, strs, lsem, wsem, wosem, dsem):
+    n, d = XF.shape
+    dt = d // T
+    KP = dt // LN
+    NP = T * KP
+    NG = NP // 4
+    F = U.shape[1]
+    FP = F // LN
+    t = lax.axis_index("tp")
+    up = lax.rem(t + 1, T)
+    dn = lax.rem(t + 3, T)
+    op = lax.rem(t + 2, T)
+    hf = n // 2
+    ALL, A, B = pl.ds(0, n), pl.ds(0, hf), pl.ds(hf, hf)
+
+    barrier = pltpu.get_barrier_semaphore()
+    for dev in (up, dn, op):
+        pl.semaphore_signal(barrier, inc=1, device_id={"tp": dev}, device_id_type=MESH)
+    pl.semaphore_wait(barrier, 3)
+
+    def rcopy(src, dst, ss, rs, dev):
+        return pltpu.make_async_remote_copy(src_ref=src, dst_ref=dst, send_sem=ss, recv_sem=rs,
+                                            device_id={"tp": dev}, device_id_type=MESH)
+
+    def pos_of(kind, k):
+        return {'own': k, 'up': KP + 2 * k, 'dn': KP + 2 * k + 1, 'op': 3 * KP + k}[kind]
+
+    order = [None] * NP
+    for kind in ('own', 'up', 'dn', 'op'):
+        for k in range(KP):
+            order[pos_of(kind, k)] = (kind, k)
+    owner_of = {'own': t, 'up': up, 'dn': dn, 'op': op}
+
+    def hloc(kind, owner, k, rows):
+        p = pos_of(kind, k)
+        return H.at[p // 4, rows, pl.ds((p % 4) * LN, LN)]
+
+    def xloc(kind, owner, k, rows):
+        return XF.at[rows, pl.ds(pl.multiple_of(owner * dt + k * LN, LN), LN)]
+
+    class Gather:
+        def __init__(self, loc):
+            self.loc = loc
+
+        def c_up(self, k):
+            return rcopy(self.loc('own', t, k, ALL), self.loc('dn', t, k, ALL), ags.at[0, k], agr.at[0, k], up)
+
+        def c_dn(self, k):
+            return rcopy(self.loc('own', t, k, ALL), self.loc('up', t, k, ALL), ags.at[1, k], agr.at[1, k], dn)
+
+        def r_up(self, k):
+            return rcopy(self.loc('dn', dn, k, A), self.loc('op', dn, k, A), ags.at[2, k], agr.at[2, k], up)
+
+        def r_dn(self, k):
+            return rcopy(self.loc('up', up, k, B), self.loc('op', up, k, B), ags.at[3, k], agr.at[3, k], dn)
+
+        def send(self, k):
+            self.c_up(k).start()
+            self.c_dn(k).start()
+
+        def wait(self, kind, k):
+            if kind == 'dn':
+                rcopy(self.loc('dn', dn, k, ALL), self.loc('dn', dn, k, ALL), ags.at[0, k], agr.at[0, k], up).wait_recv()
+                self.r_up(k).start()
+            elif kind == 'up':
+                rcopy(self.loc('up', up, k, ALL), self.loc('up', up, k, ALL), ags.at[1, k], agr.at[1, k], dn).wait_recv()
+                self.r_dn(k).start()
+            elif kind == 'op':
+                rcopy(self.loc('op', op, k, A), self.loc('op', op, k, A), ags.at[2, k], agr.at[2, k], up).wait_recv()
+                rcopy(self.loc('op', op, k, B), self.loc('op', op, k, B), ags.at[3, k], agr.at[3, k], dn).wait_recv()
+
+        def done(self):
+            for k in range(KP):
+                self.c_up(k).wait_send()
+                self.c_dn(k).wait_send()
+                self.r_up(k).wait_send()
+                self.r_dn(k).wait_send()
+
+    gh = Gather(hloc)
+    gx = Gather(xloc)
+
+    def wait_group(gather, j):
+        for kind, k in order[4 * j:4 * j + 4]:
+            gather.wait(kind, k)
+
+    def own_in(k):
+        return pltpu.make_async_copy(attn_ref.at[:, pl.ds(k * LN, LN)], hloc('own', t, k, ALL), lsem.at[0])
+
+    for k in range(KP):
+        own_in(k).start()
+    xin = pltpu.make_async_copy(x_ref.at[:, pl.ds(pl.multiple_of(t * dt, LN), dt)], xm, lsem.at[1])
+    xin.start()
+    for k in range(KP):
+        own_in(k).wait()
+    for k in range(KP):
+        gh.send(k)
+
+    per = F // dt
+    SR = wo_ref.shape[4]
+    NS = wo_ref.shape[0]
+
+    def wo_copy(p, s):
+        kind, k = order[p]
+        j = p // 4
+        return pltpu.make_async_copy(
+            wo_ref.at[s, owner_of[kind], layer, k],
+            ring.at[j // per, pl.ds((p % 4) * LN + s * SR, SR), pl.ds((j % per) * dt, dt)], wosem.at[j])
+
+    for p in range(NP):
+        for s in range(NS):
+            wo_copy(p, s).start()
+
+    def w_copy(i, q, slot):
+        p = (i // 2) * 4 + q
+        own = p < KP
+        pair = jnp.logical_and(p >= KP, p < 3 * KP)
+        k = jnp.where(own, p, jnp.where(pair, (p - KP) // 2, p - 3 * KP))
+        who = jnp.where(own, t, jnp.where(pair, jnp.where(lax.rem(p - KP, 2) == 0, up, dn), op))
+        row = pl.multiple_of(who * dt + k * LN, LN)
+        src = wg_ref if False else None
+        return row
+
+    def w_start(i, slot):
+        for q in range(4):
+            row = w_copy(i, q, slot)
+            dst = ring.at[slot, pl.ds(q * LN, LN), :]
+
+            @pl.when(lax.rem(i, 2) == 0)
+            def _():
+                pltpu.make_async_copy(wg_ref.at[layer, pl.ds(row, LN), :], dst, wsem.at[slot]).start()
+
+            @pl.when(lax.rem(i, 2) == 1)
+            def _():
+                pltpu.make_async_copy(wu_ref.at[layer, pl.ds(row, LN), :], dst, wsem.at[slot]).start()
+
+    def w_wait(slot):
+        pltpu.make_async_copy(wg_ref.at[layer, pl.ds(0, 4 * LN), :], ring.at[slot], wsem.at[slot]).wait()
+
+    NSLOT = ring.shape[0]
+    free = list(range((NG + per - 1) // per, NSLOT))
+    for s in free:
+        w_start(jnp.int32(s), s)
+
+    def zero(j, c):
+        acc[j] = jnp.zeros(acc.shape[1:], acc.dtype)
+        return c
+
+    lax.fori_loop(0, 2 * FP, zero, 0)
+
+    def wo_step(j, c):
+        for jj in range(NG):
+            @pl.when(j == jj)
+            def _():
+                wait_group(gh, jj)
+                pltpu.make_async_copy(wo_ref.at[0, 0, layer, 0], ring.at[0, pl.ds(0, SR), pl.ds(0, dt)],
+                                      wosem.at[jj]) if False else None
+                for q in range(4):
+                    for s in range(NS):
+                        wo_copy(4 * jj + q, s).wait()
+        w = ring[j // per, :, pl.ds(pl.multiple_of(lax.rem(j, per) * dt, LN), dt)]
+        r = mm(H[j], w)
+        for k in range(KP):
+            acc[k] += r[:, k * LN:(k + 1) * LN]
+        return c
+
+    lax.fori_loop(0, NG, wo_step, 0)
+    for s in range(min(NSLOT, 2 * NG)):
+        if s not in free:
+            w_start(jnp.int32(s), s)
+    gh.done()
+    xin.wait()
+    ss = jnp.zeros((n, LN), jnp.float32)
+    for k in range(KP):
+        v = xm[:, k * LN:(k + 1) * LN] + acc[k].astype(jnp.bfloat16)
+        xm[:, k * LN:(k + 1) * LN] = v
+        vf = v.astype(jnp.float32)
+        ss = ss + vf * vf
+        acc[k] = jnp.zeros(acc.shape[1:], acc.dtype)
+    sb = jnp.broadcast_to(jnp.sum(ss, axis=1, keepdims=True), (n, LN))
+    st[...] = jnp.swapaxes(sb, 0, 1)[:8]
+
+    def s_copy(j, dev):
+        return rcopy(st, strv.at[j], sts.at[j], strs.at[j], dev)
+
+    peers = ((0, up), (1, dn), (2, op))
+    for j, dev in peers:
+        s_copy(j, dev).start()
+    for j, dev in peers:
+        s_copy(j, dev).wait_recv()
+    tot = st[...] + strv[0] + strv[1] + strv[2]
+    r8 = lax.rsqrt(tot / d + EPS)
+    rb = jnp.swapaxes(jnp.concatenate([r8] * (LN // 8), axis=0), 0, 1)
+    for k in range(KP):
+        gk = g_ref[0, pl.ds(pl.multiple_of(t * dt + k * LN, LN), LN)].astype(jnp.float32)
+        hv = (xm[:, k * LN:(k + 1) * LN].astype(jnp.float32) * rb * gk[None, :]).astype(jnp.bfloat16)
+        H[k // 4, :, (k % 4) * LN:(k % 4 + 1) * LN] = hv
+    for k in range(KP):
+        gh.send(k)
+    for j, dev in peers:
+        s_copy(j, dev).wait_send()
+
+    def gu_step(i, c):
+        j = i // 2
+        slot = lax.rem(i, NSLOT)
+        for jj in range(NG):
+            @pl.when(i == 2 * jj)
+            def _():
+                wait_group(gh, jj)
+        w_wait(slot)
+        base = lax.rem(i, 2) * FP
+        for f in range(0, FP, 4):
+            m = min(4, FP - f)
+            r = mm(H[j], ring[slot, :, f * LN:(f + m) * LN])
+            for q in range(m):
+                acc[base + f + q] += r[:, q * LN:(q + 1) * LN]
+
+        @pl.when(i + NSLOT < 2 * NG)
+        def _():
+            w_start(i + NSLOT, slot)
+        return c
+
+    def d_col(p):
+        c = p // KP
+        who = jnp.where(c == 0, op, jnp.where(c == 1, up, jnp.where(c == 2, dn, t)))
+        return pl.multiple_of(who * dt + lax.rem(p, KP) * LN, LN)
+
+    def d_start(i, slot):
+        for q in range(2):
+            pltpu.make_async_copy(wd_ref.at[layer, :, pl.ds(d_col(2 * i + q), LN)],
+                                  wdb.at[slot, :, pl.ds(q * LN, LN)], dsem.at[slot]).start()
+
+    def d_wait(slot):
+        pltpu.make_async_copy(wd_ref.at[layer, :, pl.ds(0, 2 * LN)], wdb.at[slot], dsem.at[slot]).wait()
+
+    d_start(jnp.int32(0), 0)
+    d_start(jnp.int32(1), 1)
+    lax.fori_loop(0, 2 * NG, gu_step, 0)
+
+    def silu(f, c):
+        a = acc[f].astype(jnp.bfloat16).astype(jnp.float32)
+        b = acc[FP + f].astype(jnp.bfloat16).astype(jnp.float32)
+        U[:, pl.ds(pl.multiple_of(f * LN, LN), LN)] = (a * (1.0 / (1.0 + jnp.exp(-a))) * b).astype(jnp.bfloat16)
+        return c
+
+    lax.fori_loop(0, FP, silu, 0)
+    gh.done()
+
+    def c_opA(k):
+        return rcopy(acc.at[k, A, :], RA.at[k], rss.at[0, k], rsr.at[0, k], up)
+
+    def c_opB(k):
+        return rcopy(acc.at[k, B, :], RB.at[k], rss.at[1, k], rsr.at[1, k], dn)
+
+    def c_upB(k):
+        return rcopy(acc.at[KP + k, B, :], RD.at[k, B, :], rss.at[2, k], rsr.at[2, k], up)
+
+    def c_dnA(k):
+        return rcopy(acc.at[2 * KP + k, A, :], RU.at[k, A, :], rss.at[3, k], rsr.at[3, k], dn)
+
+    def c_upA(k):
+        return rcopy(acc.at[KP + k, A, :], RD.at[k, A, :], rss.at[4, k], rsr.at[4, k], up)
+
+    def c_dnB(k):
+        return rcopy(acc.at[2 * KP + k, B, :], RU.at[k, B, :], rss.at[5, k], rsr.at[5, k], dn)
+
+    def rs_send(p):
+        c = p // KP
+        k = lax.rem(p, KP)
+
+        @pl.when(c == 0)
+        def _():
+            c_opA(k).start()
+            c_opB(k).start()
+
+        @pl.when(c == 1)
+        def _():
+            c_upB(k).start()
+
+        @pl.when(c == 2)
+        def _():
+            c_dnA(k).start()
+
+    def down(i, c):
+        slot = lax.rem(i, 2)
+        d_wait(slot)
+
+        @pl.when(i > 0)
+        def _():
+            rs_send(2 * i - 2)
+            rs_send(2 * i - 1)
+
+        r = mm(U[...], wdb[slot])
+        for q in range(2):
+            acc[2 * i + q] = r[:, q * LN:(q + 1) * LN]
+
+        @pl.when(i + 2 < NP // 2)
+        def _():
+            d_start(i + 2, slot)
+        return c
+
+    lax.fori_loop(0, NP // 2, down, 0)
+
+    def add(k, c):
+        c_opA(k).wait_recv()
+        acc[KP + k, 0:hf, :] += RA[k]
+        c_upA(k).start()
+        c_opB(k).wait_recv()
+        acc[2 * KP + k, hf:n, :] += RB[k]
+        c_dnB(k).start()
+        return c
+
+    lax.fori_loop(0, KP, add, 0)
+
+    for k in range(KP):
+        c_upB(k).wait_recv()
+        c_dnA(k).wait_recv()
+        c_upA(k).wait_recv()
+        c_dnB(k).wait_recv()
+        s = acc[3 * KP + k] + RD[k] + RU[k]
+        v = xm[:, k * LN:(k + 1) * LN] + s.astype(jnp.bfloat16)
+        XF[:, pl.ds(pl.multiple_of(t * dt + k * LN, LN), LN)] = v
+        gx.send(k)
+    for k in range(KP):
+        gx.wait('up', k)
+        gx.wait('dn', k)
+    for k in range(KP):
+        gx.wait('op', k)
+    o = pltpu.make_async_copy(XF, out_ref, lsem.at[0])
+    o.start()
+    gx.done()
+    for k in range(KP):
+        for cp in (c_opA, c_opB, c_upB, c_dnA, c_upA, c_dnB):
+            cp(k).wait_send()
+    o.wait()
+
+
+def mlp(T, layer, attn, x, wo_g, g, wg, wu, wd, cid):
+    n, d = x.shape
+    F = wg.shape[2]
+    dt = d // T
+    KP = dt // LN
+    FP = F // LN
+    hf = n // 2
+    NG = T * KP // 4
+    f32, bf = jnp.float32, jnp.bfloat16
+    anyspec = pl.BlockSpec(memory_space=pltpu.HBM)
+    D = pltpu.SemaphoreType.DMA
+    return pl.pallas_call(
+        functools.partial(mlp_kernel, T, layer),
+        out_shape=jax.ShapeDtypeStruct((n, d), bf),
+        in_specs=[anyspec, anyspec, anyspec, pl.BlockSpec(memory_space=pltpu.VMEM), anyspec, anyspec, anyspec],
+        out_specs=anyspec,
+        scratch_shapes=[
+            pltpu.VMEM((2 * FP, n, LN), f32),
+            pltpu.VMEM((3, 4 * LN, F), bf),
+            pltpu.VMEM((NG, n, 4 * LN), bf),
+            pltpu.VMEM((n, F), bf),
+            pltpu.VMEM((2, F, 2 * LN), bf),
+            pltpu.VMEM((KP, hf, LN), f32),
+            pltpu.VMEM((KP, hf, LN), f32),
+            pltpu.VMEM((KP, n, LN), f32),
+            pltpu.VMEM((KP, n, LN), f32),
+            pltpu.VMEM((n, d), bf),
+            pltpu.VMEM((n, dt), bf),
+            pltpu.VMEM((8, n), f32),
+            pltpu.VMEM((3, 8, n), f32),
+            D((4, KP)), D((4, KP)), D((6, KP)), D((6, KP)), D((3,)), D((3,)),
+            D((2,)), D((3,)), D((NG,)), D((2,)),
+        ],
+        compiler_params=pltpu.CompilerParams(vmem_limit_bytes=61 * 2 ** 20, collective_id=cid, has_side_effects=True),
+        cost_estimate=pl.CostEstimate(flops=2 * n * d * (3 * F + dt), bytes_accessed=2 * d * (3 * F + dt), transcendentals=n * F),
+        name="mlp",
+    )(attn, x, wo_g, g, wg, wu, wd)
 
 
 def solution(mesh):
@@ -159,15 +540,23 @@
         layers, hc, kvl, dh = k_hist.shape
         hql = wq.shape[-1] // dh
         dt = d // tp
-        my = lax.axis_index('tp') * dt
+        tt, ss = lax.axis_index('tp'), lax.axis_index('sp')
+        kp = dt // LN
+        sr = LN // sp
+        wr = lax.dynamic_index_in_dim(wo.reshape(layers, kp, sp, sr, d), ss, axis=2, keepdims=False)
+
+        def wcols(t):
+            return lax.dynamic_slice_in_dim(wr, t * dt, dt, axis=3)
+
+        parts = jnp.zeros((tp,) + wcols(0).shape, wo.dtype)
+        parts = lax.dynamic_update_index_in_dim(parts, wcols(tt), tt, 0)
+        for j in range(1, tp):
+            got = lax.ppermute(wcols(lax.rem(tt + j, tp)), 'tp', [(i, (i + j) % tp) for i in range(tp)])
+            parts = lax.dynamic_update_index_in_dim(parts, got, lax.rem(tt + tp - j, tp), 0)
         kv = jnp.stack([k_hist[:, :, 0], v_hist[:, :, 0]], axis=1).reshape(2 * layers, hc, dh)
         hist = lax.all_gather(kv, 'sp', axis=0)
         ks, vs = [], []
-
-        def reduce_add(x, part):
-            red = lax.psum_scatter(part, 'tp', scatter_dimension=1, tiled=True)
-            xc = lax.dynamic_slice_in_dim(x, my, dt, axis=1) + red.astype(jnp.bfloat16)
-            return lax.all_gather(xc, 'tp', axis=1, tiled=True)
+        wo_g = None
 
         for l in range(layers):
             h = rmsnorm(x, g1[l])
@@ -176,14 +565,11 @@
             ks.append(k)
             vs.append(v)
             new = lax.all_gather(jnp.stack([k[:, 0], v[:, 0]]), 'sp', axis=0)
+            if wo_g is None:
+                wo_g = lax.all_gather(parts, 'sp', axis=0)
             q = rope(mm(h, wq[l]).astype(jnp.bfloat16).reshape(n, hql, dh), pos)
             attn = attention(sp, l, q.reshape(n, hql * dh), hist, new)
-            x = reduce_add(x, mm(attn, wo[l]))
-            h2 = rmsnorm(x, g2[l])
-            a = mm(h2, wg[l]).astype(jnp.bfloat16)
-            b = mm(h2, wu[l]).astype(jnp.bfloat16)
-            u = (jax.nn.silu(a.astype(jnp.float32)) * b.astype(jnp.float32)).astype(jnp.bfloat16)
-            x = reduce_add(x, mm(u, wd[l]))
+            x = mlp(tp, l, attn, x, wo_g, g2[l:l + 1], wg, wu, wd, l)
         return x, jnp.stack(ks), jnp.stack(vs)
 
     in_specs = (P(row, None), P(row), kv_spec, kv_spec, col, col, col, rowsplit, col, col, rowsplit, P(), P())

time: 954 us -> 648 us (0.68)
  the two profiles are of different devices: /device:TPU:100 before, /device:TPU:103 now
where the time goes in v2:
time: 648 us; the launch traced here: 642 us
  Pallas kernels  511 us (79%)
  waiting for transfers between devices  52.5 us (8%)
  matrix products  26.9 us (4%)
  local copies, waits for them, and re-layouts  21.2 us (3%)
  between operations  14.3 us (2%)
  other arithmetic  9.51 us (1%)
  starting transfers between devices  6.5 us (1%)
    pallas_call x2, Pallas kernels, mlp(): pl.pallas_call(functools.partial(mlp_kernel, T, layer), out_shape=jax.Sha...  351 us
    pallas_call x2, Pallas kernels, attention(): pl.pallas_call(functools.partial(attn_kernel, sp, layer), out_shape=jax.S...  160 us
    all_gather x1, waiting for transfers between devices, body(): hist = lax.all_gather(kv, 'sp', axis=0)  30.2 us
    dot_general x6, matrix products, mm(): return jnp.dot(a, b, preferred_element_type=jnp.float32)  26.9 us
    ppermute x3, waiting for transfers between devices, body(): lax.ppermute(wcols(lax.rem(tt + j, tp)), 'tp', [(i, (i + j) % tp) for i i...  15.5 us
  transfers between devices with their start and end apart: 7, of which 4 were waited for; matrix products, arithmetic and copies ran while one was open for 5% of the time, Pallas kernels for 12%

profile of v2, /device:TPU:103, one launch (start us, length us, event | category | flops | bytes accessed | tf_op | source)
XLA Modules:
  0.0 642.1 jit_solution(1068153405456496844)
XLA Ops:
  8.2 3.0 fusion
  11.3 2.8 convolution_convert_fusion.2
  14.1 1.5 fusion.25
  18.6 3.0 dynamic-slice_bitcast_fusion
  21.6 1.8 collective-permute-start
  23.4 3.7 collective-permute-start.1
  29.0 6.1 collective-permute-done
  35.1 9.4 %collective-permute-done.1 = bf16[2,7,16,896]{3,2,1,0:T(8,128)(2,1)S(1)} collective-permute-done((bf16[2,7,16,896]{3,2,1,0:T(8,128)(2,1)}, bf16[2,7,16,896]{3,2,1,0:T(8,128)(2,1)S(1)}, u32[]{:S(2)}, u32[]{:S(2)}) %collective-permute-start.1) | collective-permute-done | bytes 401440 | tf_op jit(solution)/shard_map/ppermute | solution.py:554
  46.1 9.2 %fusion.15 = f32[512,896]{1,0:T(8,128)} fusion(bf16[2,3584,896]{2,1,0:T(8,128)(2,1)} %param.17, bf16[512,3584]{1,0:T(8,128)(2,1)} %x_ref.1, f32[3584]{0:T(1024)S(1)} %get-tuple-element.13, f32[512]{0:T(512)S(1)} %add_rsqrt_fusion.1), kind=kOutput, calls=%fused_computation.17 | convolution fusion | flops 3296591872 | bytes 11943936 | tf_op jit(solution)/shard_map/dot_general | solution.py:34
  55.3 1.8 copy.42
  58.0 1.3 copy.46.q_ref
  59.9 30.2 %all-gather.7.cloned.1.call-done.hist_ref = bf16[8,4,1024,128]{3,2,1,0:T(8,128)(2,1)} async-done(((bf16[1,4,1024,128]{3,2,1,0:T(8,128)(2,1)}), bf16[8,4,1024,128]{3,2,1,0:T(8,128)(2,1)}) %all-gather.7.cloned.1.call-update) | async-done | bytes 8388624 | tf_op jit(solution)/shard_map/all_gather | solution.py:557
  90.1 80.0 %attention.2.attn_ref = bf16[512,896]{1,0:T(8,128)(2,1)} custom-call(bf16[512,896]{1,0:T(8,128)(2,1)} %copy.46.q_ref, bf16[8,4,1024,128]{3,2,1,0:T(8,128)(2,1)} %all-gather.7.cloned.1.call-done.hist_ref, bf16[8,2,512,128]{3,2,1,0:T(8,128)(2,1)} %bitcast.101), custom_call_target="tpu_custom_call" | custom-call | flops 18790481920 | bytes 5242880 | tf_op jit(solution)/shard_map/attention/pallas_call | solution.py:128
  170.1 175.8 %mlp.2.x_ref = bf16[512,3584]{1,0:T(8,128)(2,1)} custom-call(bf16[512,896]{1,0:T(8,128)(2,1)} %attention.2.attn_ref, bf16[512,3584]{1,0:T(8,128)(2,1)} %x_ref.1, bf16[8,4,2,7,16,896]{5,4,3,2,1,0:T(8,128)(2,1)} %all-gather.9.cloned.1.call-done.wo_ref, bf16[1,3584]{1,0:T(2,128)(2,1)} %get-tuple-element.26.g_ref, bf16[2,3584,4736]{2,1,0:T(8,128)(2,1)} %wg_ref.3, ...), custom_call_target="tpu_custom_call" | custom-call | flops 55431921664 | bytes 108265472 | tf_op jit(solution)/shard_map/mlp/pallas_call | solution.py:502
  345.9 3.0 fusion.3
  349.1 2.8 convolution_convert_fusion
  351.9 1.5 fusion.27
  354.8 9.2 %fusion.21 = f32[512,896]{1,0:T(8,128)} fusion(bf16[2,3584,896]{2,1,0:T(8,128)(2,1)} %param.17, bf16[512,3584]{1,0:T(8,128)(2,1)} %mlp.2.x_ref, f32[3584]{0:T(1024)S(1)} %get-tuple-element.12, f32[512]{0:T(512)S(1)} %add_rsqrt_fusion), kind=kOutput, calls=%fused_computation.19 | convolution fusion | flops 3296591872 | bytes 11943936 | tf_op jit(solution)/shard_map/dot_general | solution.py:34
  364.0 1.8 copy.51
  366.2 1.3 copy.54.q_ref
  369.2 6.6 %all-gather.13.cloned.1.call-done = bf16[16,512,128]{2,1,0:T(8,128)(2,1)} async-done(((bf16[2,512,128]{2,1,0:T(8,128)(2,1)}), bf16[16,512,128]{2,1,0:T(8,128)(2,1)}) %all-gather.13.cloned.1.call-update) | async-done | bytes 2097168 | tf_op jit(solution)/shard_map/all_gather | solution.py:567
  375.8 79.8 %attention.3.attn_ref = bf16[512,896]{1,0:T(8,128)(2,1)} custom-call(bf16[512,896]{1,0:T(8,128)(2,1)} %copy.54.q_ref, bf16[8,4,1024,128]{3,2,1,0:T(8,128)(2,1)} %all-gather.7.cloned.1.call-done.hist_ref, bf16[8,2,512,128]{3,2,1,0:T(8,128)(2,1)} %bitcast.102), custom_call_target="tpu_custom_call" | custom-call | flops 18790481920 | bytes 5242880 | tf_op jit(solution)/shard_map/attention/pallas_call | solution.py:128
  455.6 175.6 %mlp.3 = bf16[512,3584]{1,0:T(8,128)(2,1)} custom-call(bf16[512,896]{1,0:T(8,128)(2,1)} %attention.3.attn_ref, bf16[512,3584]{1,0:T(8,128)(2,1)} %mlp.2.x_ref, bf16[8,4,2,7,16,896]{5,4,3,2,1,0:T(8,128)(2,1)} %all-gather.9.cloned.1.call-done.wo_ref, bf16[1,3584]{1,0:T(2,128)(2,1)} %get-tuple-element.25.g_ref, bf16[2,3584,4736]{2,1,0:T(8,128)(2,1)} %wg_ref.3, ...), custom_call_target="tpu_custom_call" | custom-call | flops 55431921664 | bytes 108265472 | tf_op jit(solution)/shard_map/mlp/pallas_call | solution.py:502
  631.3 4.1 copy.68
  (58 shorter events, 12.7 us)
Async XLA Ops:
  7.2 4.1 copy-start.6
  7.2 52.7 %all-gather.11.cloned.1.call-start = ((), (), s32[]{:S(2)}) async-start(), calls=%async_computation.2 | async-start | bytes 2359296 | tf_op jit(solution)/shard_map/all_gather | solution.py:567
  7.3 4.0 copy-start.1
  11.3 2.8 copy-start.7
  14.1 3.1 copy-start.3
  14.1 3.1 copy-start.4
  17.1 73.0 %all-gather.7.cloned.1.call-start = ((), (), s32[]{:S(2)}) async-start(), calls=%async_computation | async-start | bytes 9437184 | tf_op jit(solution)/shard_map/all_gather | solution.py:557
  18.5 151.6 %all-gather.9.cloned.1.call-start = ((), (), s32[]{:S(2)}) async-start(), calls=%async_computation.1 | async-start | bytes 14450688 | tf_op jit(solution)/shard_map/all_gather | solution.py:569
  21.6 13.5 %collective-permute-start = (bf16[2,7,16,896]{3,2,1,0:T(8,128)(2,1)}, bf16[2,7,16,896]{3,2,1,0:T(8,128)(2,1)S(1)}, u32[]{:S(2)}, u32[]{:S(2)}) collective-permute-start(bf16[2,7,16,896]{3,2,1,0:T(8,128)(2,1)} %get-tuple-element.16), channel_id=1, source_target_pairs={{0,8},{8,16},{16,24},{24,0},{1,9},{9,17},{17,25},{25,1},{2,10},{10... | collective-permute-start | bytes 1204232 | tf_op jit(solution)/shard_map/ppermute | solution.py:554
  23.4 21.1 %collective-permute-start.1 = (bf16[2,7,16,896]{3,2,1,0:T(8,128)(2,1)}, bf16[2,7,16,896]{3,2,1,0:T(8,128)(2,1)S(1)}, u32[]{:S(2)}, u32[]{:S(2)}) collective-permute-start(bf16[2,7,16,896]{3,2,1,0:T(8,128)(2,1)} %get-tuple-element.15), channel_id=1, source_target_pairs={{0,16},{8,24},{16,0},{24,8},{1,17},{9,25},{17,1},{25,9},{2,18},{10... | collective-permute-start | bytes 1204232 | tf_op jit(solution)/shard_map/ppermute | solution.py:554
  27.1 17.4 %collective-permute-start.2 = (bf16[2,7,16,896]{3,2,1,0:T(8,128)(2,1)}, bf16[2,7,16,896]{3,2,1,0:T(8,128)(2,1)S(1)}, u32[]{:S(2)}, u32[]{:S(2)}) collective-permute-start(bf16[2,7,16,896]{3,2,1,0:T(8,128)(2,1)} %get-tuple-element.14), channel_id=1, source_target_pairs={{0,24},{8,0},{16,8},{24,16},{1,25},{9,1},{17,9},{25,17},{2,26},{10... | collective-permute-start | bytes 1204232 | tf_op jit(solution)/shard_map/ppermute | solution.py:554
  44.6 1.2 copy-start.2
  45.9 330.0 %all-gather.13.cloned.1.call-start = ((), (), s32[]{:S(2)}) async-start(), calls=%async_computation.3 | async-start | bytes 2359296 | tf_op jit(solution)/shard_map/all_gather | solution.py:567
  57.1 2.2 copy-start.5
  345.9 3.1 copy-start
  349.1 2.8 copy-start.8
Sparse Core Ops, SparseCore 0:
  17.2 24.3 all-gather.10
  43.2 46.8 all-gather.6
  91.7 66.2 all-gather.8
  355.0 20.8 all-gather.12

commit v3 on v2

--- a/solution.py
+++ b/solution.py
@@ -10,149 +10,323 @@
 EPS = 1e-5
 ROPE_THETA = 500000.0
 LOG2E = 1.4426950408889634
-
-
-def rmsnorm(x, g):
-    xf = x.astype(jnp.float32)
-    r = lax.rsqrt(jnp.mean(xf * xf, axis=-1, keepdims=True) + EPS)
-    return (xf * r * g.astype(jnp.float32)).astype(jnp.bfloat16)
-
-
-def rope(t, pos):
-    half = t.shape[-1] // 2
-    inv = ROPE_THETA ** (-(jnp.arange(half, dtype=jnp.float32) * (2.0 / t.shape[-1])))
-    ang = pos.astype(jnp.float32)[..., None] * inv
-    c = jnp.cos(ang)[..., None, :]
-    s = jnp.sin(ang)[..., None, :]
-    tf = t.astype(jnp.float32)
-    t1 = tf[..., :half]
-    t2 = tf[..., half:]
-    return jnp.concatenate([t1 * c - t2 * s, t2 * c + t1 * s], axis=-1).astype(jnp.bfloat16)
+MESH = pl.DeviceIdType.MESH
+LN = 128
 
 
 def mm(a, b):
     return jnp.dot(a, b, preferred_element_type=jnp.float32)
 
 
-def attn_kernel(sp, layer, q_ref, hist_ref, new_ref, o_ref, hkv, nkv, m_ref, l_ref, acc_ref, hsem, nsem):
-    n, w = q_ref.shape
-    dh = hkv.shape[-1]
+def attn_kernel(T, SP, layer, x_ref, cos_ref, sin_ref, kh_ref, vh_ref, wq_ref, wk_ref, wv_ref, g_ref,
+                out_ref, ko_ref, vo_ref,
+                xb, wb, kv, qb, m_ref, l_ref, acc_ref, ga,
+                kvs, kvr, gas, gar, lsem, hsem, wsem):
+    n, d = xb.shape
+    w = qb.shape[1]
+    dh = kv.shape[3]
     heads = w // dh
-    hc = hkv.shape[2]
-    nc = nkv.shape[2]
-    rows_t = min(256, n)
-    nt = n // rows_t
-    c = dh ** -0.5 * LOG2E
+    X = SP // 2
+    C = kv.shape[2]
+    hc = C // 2
+    R = min(128, n)
+    nt = n // R
+    scale = dh ** -0.5 * LOG2E
     me = lax.axis_index("sp")
-    for b in range(sp):
+    t = lax.axis_index("tp")
+    c = lax.rem(me, 2)
+    xx = me // 2
+    lx, rx, ox = lax.rem(xx + X - 1, X), lax.rem(xx + 1, X), lax.rem(xx + 2, X)
+    left, right, part = lx * 2 + c, rx * 2 + c, xx * 2 + 1 - c
+    up, dn = lax.rem(t + 1, T), lax.rem(t + T - 1, T)
+
+    barrier = pltpu.get_barrier_semaphore()
+    for dev in ({"sp": left}, {"sp": right}, {"sp": part}, {"tp": up}, {"tp": dn}):
+        pl.semaphore_signal(barrier, inc=1, device_id=dev, device_id_type=MESH)
+
+    def hist_in(j):
+        return pltpu.make_async_copy((kh_ref, vh_ref)[j].at[layer], kv.at[xx, j, pl.ds(c * hc, hc), :], hsem)
+
+    for j in range(2):
+        hist_in(j).start()
+    xin = pltpu.make_async_copy(x_ref, xb, lsem.at[0])
+    xin.start()
+    win = [pltpu.make_async_copy(wk_ref.at[layer], wb.at[:, 0:dh], wsem.at[0]),
+           pltpu.make_async_copy(wv_ref.at[layer], wb.at[:, dh:2 * dh], wsem.at[0]),
+           pltpu.make_async_copy(wq_ref.at[layer], wb.at[:, 2 * dh:], wsem.at[1])]
+    for cp in win:
+        cp.start()
+
+    def region(kind, chip, core, half):
+        if kind == 0:
+            blk, base, ln = chip, core * hc, hc
+        else:
+            blk, base, ln = X + chip // 2, lax.rem(chip, 2) * (2 * n) + core * n, n
+        if half is not None:
+            ln = ln // 2
+            base = base + half * ln
+        return kv.at[blk, :, pl.ds(pl.multiple_of(base, ln), ln), :]
+
+    sent = [(xx, c, None, right), (xx, c, None, left), (xx, c, None, part), (lx, c, 0, right), (rx, c, 1, left),
+            (lx, c, None, part), (rx, c, None, part), (ox, c, 0, part), (ox, c, 1, part)]
+    got = [(lx, c, None), (rx, c, None), (xx, 1 - c, None), (ox, c, 0), (ox, c, 1),
+           (lx, 1 - c, None), (rx, 1 - c, None), (ox, 1 - c, 0), (ox, 1 - c, 1)]
+
+    def tx(kind, i):
+        chip, core, half, dev = sent[i]
+        r = region(kind, chip, core, half)
+        return pltpu.make_async_remote_copy(src_ref=r, dst_ref=r, send_sem=kvs.at[kind, i], recv_sem=kvr.at[kind, i],
+                                            device_id={"sp": dev}, device_id_type=MESH)
+
+    def rx_wait(kind, i):
+        chip, core, half = got[i]
+        r = region(kind, chip, core, half)
+        pltpu.make_async_remote_copy(src_ref=r, dst_ref=r, send_sem=kvs.at[kind, i], recv_sem=kvr.at[kind, i],
+                                     device_id={"sp": part}, device_id_type=MESH).wait_recv()
+
+    def send_own(kind):
+        for i in (0, 1, 2):
+            tx(kind, i).start()
+
+    def pass_near(kind):
+        rx_wait(kind, 0)
+        tx(kind, 3).start()
+        tx(kind, 5).start()
+        rx_wait(kind, 1)
+        tx(kind, 4).start()
+        tx(kind, 6).start()
+
+    def pass_far(kind):
+        rx_wait(kind, 3)
+        tx(kind, 7).start()
+        rx_wait(kind, 4)
+        tx(kind, 8).start()
+
+    pl.semaphore_wait(barrier, 5)
+    for j in range(2):
+        hist_in(j).wait()
+    send_own(0)
+
+    xin.wait()
+    g = g_ref[...].astype(jnp.float32)
+    NR = min(32, n)
+
+    def norm(i, carry):
+        rows = pl.ds(pl.multiple_of(i * NR, NR), NR)
+        xf = xb[rows, :].astype(jnp.float32)
+        r = lax.rsqrt(jnp.sum(xf * xf, axis=1, keepdims=True) / d + EPS)
+        xb[rows, :] = (xf * r * g).astype(jnp.bfloat16)
+        return carry
+
+    lax.fori_loop(0, n // NR, norm, 0)
+
+    def rope(a):
+        a = a.astype(jnp.bfloat16).astype(jnp.float32)
+        return (a * cos_ref[...] + pltpu.roll(a, dh // 2, 1) * sin_ref[...]).astype(jnp.bfloat16)
+
+    win[0].wait()
+    win[1].wait()
+    r = mm(xb[...], wb[:, :2 * dh])
+    own = pl.ds(pl.multiple_of(lax.rem(xx, 2) * (2 * n) + c * n, n), n)
+    kv[X + xx // 2, 0, own, :] = rope(r[:, :dh])
+    kv[X + xx // 2, 1, own, :] = r[:, dh:].astype(jnp.bfloat16)
+    win[2].wait()
+
+    def qpair(i, carry):
+        @pl.when(i == 1)
+        def _():
+            send_own(1)
+
+        r = mm(xb[...], wb[:, pl.ds(pl.multiple_of((i + 1) * 2 * dh, 2 * dh), 2 * dh)])
         for j in range(2):
-            pltpu.make_async_copy(hist_ref.at[b, 2 * layer + j], hkv.at[b, j], hsem.at[b, j]).start()
-    for b in range(sp):
-        pltpu.make_async_copy(new_ref.at[b], nkv.at[b], nsem.at[b]).start()
-    m_ref[...] = jnp.full(m_ref.shape, -1e30, jnp.float32)
-    l_ref[...] = jnp.zeros_like(l_ref)
-    acc_ref[...] = jnp.zeros_like(acc_ref)
-
-    def block(t, k_of, v_of, cols, mask):
-        rows = pl.ds(pl.multiple_of(t * rows_t, rows_t), rows_t)
-
-        def qk(g):
-            return lax.dot_general(q_ref[rows, g * dh:(g + 1) * dh], k_of(), (((1,), (1,)), ((), ())),
+            qb[:, pl.ds(pl.multiple_of((2 * i + j) * dh, dh), dh)] = rope(r[:, j * dh:(j + 1) * dh])
+        return carry
+
+    lax.fori_loop(0, heads // 2, qpair, 0)
+    if heads // 2 < 2:
+        send_own(1)
+    if heads % 2:
+        qb[:, (heads - 1) * dh:] = rope(mm(xb[...], wb[:, (heads + 1) * dh:]))
+
+    def kv_out(j):
+        return pltpu.make_async_copy(kv.at[X + xx // 2, j, own, :], (ko_ref, vo_ref)[j], hsem)
+
+    for j in range(2):
+        kv_out(j).start()
+
+    def init(i, carry):
+        rows = pl.ds(pl.multiple_of(i * R, R), R)
+        for h in range(heads):
+            m_ref[h, rows, :] = jnp.full((R, LN), -1e30, jnp.float32)
+            l_ref[h, rows, :] = jnp.zeros((R, LN), jnp.float32)
+            acc_ref[h, rows, :] = jnp.zeros((R, dh), jnp.float32)
+        return carry
+
+    lax.fori_loop(0, nt, init, 0)
+
+    def unit(tile, blk, mask):
+        rows = pl.ds(pl.multiple_of(tile * R, R), R)
+
+        def qk(h):
+            return lax.dot_general(qb[rows, h * dh:(h + 1) * dh], kv[blk, 0], (((1,), (1,)), ((), ())),
                                    preferred_element_type=jnp.float32)
+
+        def pv(h, p, alpha):
+            acc_ref[h, rows, :] = acc_ref[h, rows, :] * alpha + mm(p, kv[blk, 1])
 
         s = qk(0)
         pend = None
-
-        def pv(g, p, alpha):
-            acc_ref[g, rows, :] = acc_ref[g, rows, :] * alpha + mm(p, v_of())
-
-        for g in range(heads):
-            s_next = qk(g + 1) if g + 1 < heads else None
+        for h in range(heads):
+            s_next = qk(h + 1) if h + 1 < heads else None
             if pend is not None:
                 pv(*pend)
             if mask is not None:
                 s = jnp.where(mask, s, -jnp.inf)
-            m_old = m_ref[g, rows, :]
-            m_new = jnp.maximum(m_old, jnp.max(s, axis=1, keepdims=True) * c)
+            m_old = m_ref[h, rows, :]
+            m_new = jnp.maximum(m_old, jnp.max(s, axis=1, keepdims=True) * scale)
             alpha = jnp.exp2(m_old - m_new)
-            p = jnp.exp2(s * c - m_new[:, :1])
-            ls = p[:, :dh]
-            for j in range(1, cols // dh):
-                ls = ls + p[:, j * dh:(j + 1) * dh]
-            l_ref[g, rows, :] = l_ref[g, rows, :] * alpha + ls
-            m_ref[g, rows, :] = m_new
-            pend = (g, p.astype(jnp.bfloat16), alpha)
+            p = jnp.exp2(s * scale - m_new[:, :1])
+            ls = p[:, :LN]
+            for j in range(1, C // LN):
+                ls = ls + p[:, j * LN:(j + 1) * LN]
+            l_ref[h, rows, :] = l_ref[h, rows, :] * alpha + ls
+            m_ref[h, rows, :] = m_new
+            pend = (h, p.astype(jnp.bfloat16), alpha)
             s = s_next
         pv(*pend)
 
-    def hist_body(i, carry):
-        b = i // nt
-        t = i % nt
-
-        @pl.when(t == 0)
-        def _():
-            for j in range(2):
-                pltpu.make_async_copy(hist_ref.at[b, 2 * layer + j], hkv.at[b, j], hsem.at[b, j]).wait()
-
-        block(t, lambda: hkv[b, 0], lambda: hkv[b, 1], hc, None)
+    hR = R // 2
+
+    def gx(i, tile):
+        base = pl.multiple_of(tile * R, R)
+        owner, off, ln, dev = ((t, 0, R, up), (t, 0, R, dn), (dn, 0, hR, up), (up, hR, hR, dn))[i]
+        ref = ga.at[owner, pl.ds(pl.multiple_of(base + off, hR), ln), :]
+        return pltpu.make_async_remote_copy(src_ref=ref, dst_ref=ref, send_sem=gas.at[i, tile], recv_sem=gar.at[i, tile],
+                                            device_id={"tp": dev}, device_id_type=MESH)
+
+    def g_wait(i, tile):
+        base = pl.multiple_of(tile * R, R)
+        far = lax.rem(t + 2, T)
+        owner, off, ln = ((dn, 0, R), (up, 0, R), (far, 0, hR), (far, hR, hR))[i]
+        ref = ga.at[owner, pl.ds(pl.multiple_of(base + off, hR), ln), :]
+        pltpu.make_async_remote_copy(src_ref=ref, dst_ref=ref, send_sem=gas.at[i, tile], recv_sem=gar.at[i, tile],
+                                     device_id={"tp": up}, device_id_type=MESH).wait_recv()
+
+    def g_pass(tile):
+        g_wait(0, tile)
+        gx(2, tile).start()
+        g_wait(1, tile)
+        gx(3, tile).start()
+
+    def finish(tile):
+        rows = pl.ds(pl.multiple_of(tile * R, R), R)
+        for h in range(heads):
+            l = jnp.sum(l_ref[h, rows, :], axis=1, keepdims=True)
+            ga[t, rows, h * dh:(h + 1) * dh] = (acc_ref[h, rows, :] / l).astype(jnp.bfloat16)
+
+    rx_wait(0, 2)
+    first = 3 * nt
+    per = 1 + xx // 2
+    pts = [2, nt, 2 * nt - 2, 2 * nt] if nt >= 4 else [0, 1, 2, 3]
+
+    def step(i, carry):
+        for at, fn, kind in zip(pts, (pass_near, pass_near, pass_far, pass_far), (0, 1, 0, 1)):
+            @pl.when(i == at)
+            def _():
+                fn(kind)
+
+        for chip_at, gid in ((nt, 5), (2 * nt, 6)):
+            @pl.when(i == chip_at)
+            def _():
+                rx_wait(0, gid)
+
+        @pl.when(i == first)
+        def _():
+            rx_wait(0, 7)
+            rx_wait(0, 8)
+            for gid in (2, 5, 6, 7, 8):
+                rx_wait(1, gid)
+
+        late = i >= first
+        i2 = jnp.maximum(i - first, 0)
+        m = lax.rem(i2, per)
+        tile = jnp.where(late, i2 // per, lax.rem(i, nt))
+        early = jnp.where(i < nt, xx, jnp.where(i < 2 * nt, lx, rx))
+        blk = jnp.where(late, jnp.where(m == 0, ox, X + m - 1), early)
+        unit(tile, blk, None)
+
+        @pl.when(jnp.logical_and(late, jnp.logical_and(m == 0, tile >= 2)))
+        def _():
+            g_pass(tile - 2)
+
+        @pl.when(jnp.logical_and(late, m == per - 1))
+        def _():
+            off = lax.rem(xx, 2) * (2 * n) + c * n + tile * R
+            row = lax.broadcasted_iota(jnp.int32, (R, C), 0) + off
+            unit(tile, X + xx // 2, lax.broadcasted_iota(jnp.int32, (R, C), 1) <= row)
+            finish(tile)
+            gx(0, tile).start()
+            gx(1, tile).start()
         return carry
 
-    lax.fori_loop(0, sp * nt, hist_body, 0)
-    for b in range(sp):
-        pltpu.make_async_copy(new_ref.at[b], nkv.at[b], nsem.at[b]).wait()
-
-    def new_body(i, carry):
-        b = i // nt
-        block(i % nt, lambda: nkv[b, 0], lambda: nkv[b, 1], nc, None)
-        return carry
-
-    lax.fori_loop(0, me * nt, new_body, 0)
-
-    def diag_body(t, carry):
-        r = lax.broadcasted_iota(jnp.int32, (rows_t, nc), 0) + t * rows_t
-        col = lax.broadcasted_iota(jnp.int32, (rows_t, nc), 1)
-        block(t, lambda: nkv[me, 0], lambda: nkv[me, 1], nc, col <= r)
-        return carry
-
-    lax.fori_loop(0, nt, diag_body, 0)
-    for g in range(heads):
-        l = jnp.sum(l_ref[g], axis=1, keepdims=True)
-        o_ref[:, g * dh:(g + 1) * dh] = (acc_ref[g] / l).astype(jnp.bfloat16)
-
-
-def attention(sp, layer, q, hist, new):
-    n, w = q.shape
-    _, _, hc, dh = hist.shape
+    lax.fori_loop(0, first + nt * per, step, 0)
+    for tile in range(max(nt - 2, 0), nt):
+        g_pass(tile)
+    for tile in range(nt):
+        g_wait(2, tile)
+        g_wait(3, tile)
+    o = pltpu.make_async_copy(ga, out_ref, lsem.at[0])
+    o.start()
+    for tile in range(nt):
+        for i in range(4):
+            gx(i, tile).wait_send()
+    for kind in range(2):
+        for i in range(9):
+            tx(kind, i).wait_send()
+    for j in range(2):
+        kv_out(j).wait()
+    o.wait()
+
+
+def attention(T, SP, layer, x, cos, sin, kh, vh, wq, wk, wv, g, cid):
+    n, d = x.shape
+    w = wq.shape[2]
+    hc, dh = kh.shape[1], kh.shape[2]
     heads = w // dh
-    keys = sp * hc + sp * n // 2
+    X = SP // 2
+    assert 2 * hc == 4 * n and wk.shape[2] == dh
+    R = min(128, n)
+    f32, bf = jnp.float32, jnp.bfloat16
+    hbm = pl.BlockSpec(memory_space=pltpu.HBM)
+    vm = pl.BlockSpec(memory_space=pltpu.VMEM)
+    D = pltpu.SemaphoreType.DMA
+    keys = SP * (hc + n // 2)
     return pl.pallas_call(
-        functools.partial(attn_kernel, sp, layer),
-        out_shape=jax.ShapeDtypeStruct((n, w), jnp.bfloat16),
-        in_specs=[pl.BlockSpec(memory_space=pltpu.VMEM), pl.BlockSpec(memory_space=pltpu.HBM),
-                  pl.BlockSpec(memory_space=pltpu.HBM)],
-        out_specs=pl.BlockSpec(memory_space=pltpu.VMEM),
+        functools.partial(attn_kernel, T, SP, layer),
+        out_shape=[jax.ShapeDtypeStruct((T, n, w), bf), jax.ShapeDtypeStruct((n, dh), bf), jax.ShapeDtypeStruct((n, dh), bf)],
+        in_specs=[hbm, vm, vm, hbm, hbm, hbm, hbm, hbm, vm],
+        out_specs=[hbm, hbm, hbm],
         scratch_shapes=[
-            pltpu.VMEM((sp, 2, hc, dh), jnp.bfloat16),
-            pltpu.VMEM((sp, 2, n, dh), jnp.bfloat16),
-            pltpu.VMEM((heads, n, dh), jnp.float32),
-            pltpu.VMEM((heads, n, dh), jnp.float32),
-            pltpu.VMEM((heads, n, dh), jnp.float32),
-            pltpu.SemaphoreType.DMA((sp, 2)),
-            pltpu.SemaphoreType.DMA((sp,)),
+            pltpu.VMEM((n, d), bf),
+            pltpu.VMEM((d, w + 2 * dh), bf),
+            pltpu.VMEM((X + X // 2, 2, 2 * hc, dh), bf),
+            pltpu.VMEM((n, w), bf),
+            pltpu.VMEM((heads, n, LN), f32),
+            pltpu.VMEM((heads, n, LN), f32),
+            pltpu.VMEM((heads, n, dh), f32),
+            pltpu.VMEM((T, n, w), bf),
+            D((2, 9)), D((2, 9)), D((4, n // R)), D((4, n // R)), D((2,)), D, D((2,)),
         ],
-        compiler_params=pltpu.CompilerParams(vmem_limit_bytes=60 * 2 ** 20),
-        cost_estimate=pl.CostEstimate(flops=4 * n * w * keys, bytes_accessed=4 * keys * dh, transcendentals=n * heads * keys),
+        compiler_params=pltpu.CompilerParams(vmem_limit_bytes=61 * 2 ** 20, collective_id=cid, has_side_effects=True),
+        cost_estimate=pl.CostEstimate(flops=4 * n * w * keys + 2 * n * d * (w + 2 * dh), bytes_accessed=4 * keys * dh,
+                                      transcendentals=n * heads * keys),
         name="attention",
-    )(q, hist, new)
-
-
-MESH = pl.DeviceIdType.MESH
-LN = 128
+    )(x, cos, sin, kh, vh, wq, wk, wv, g)
 
 
 def mlp_kernel(T, layer, attn_ref, x_ref, wo_ref, g_ref, wg_ref, wu_ref, wd_ref, out_ref,
                acc, ring, H, U, wdb, RA, RB, RD, RU, XF, xm, st, strv,
-               ags, agr, rss, rsr, sts, strs, lsem, wsem, wosem, dsem):
+               ags, agr, rss, rsr, sts, strs, lsem, wsem, wosem, dsem, hsem):
     n, d = XF.shape
     dt = d // T
     KP = dt // LN
@@ -170,7 +344,6 @@
     barrier = pltpu.get_barrier_semaphore()
     for dev in (up, dn, op):
         pl.semaphore_signal(barrier, inc=1, device_id={"tp": dev}, device_id_type=MESH)
-    pl.semaphore_wait(barrier, 3)
 
     def rcopy(src, dst, ss, rs, dev):
         return pltpu.make_async_remote_copy(src_ref=src, dst_ref=dst, send_sem=ss, recv_sem=rs,
@@ -237,17 +410,14 @@
         for kind, k in order[4 * j:4 * j + 4]:
             gather.wait(kind, k)
 
-    def own_in(k):
-        return pltpu.make_async_copy(attn_ref.at[:, pl.ds(k * LN, LN)], hloc('own', t, k, ALL), lsem.at[0])
-
-    for k in range(KP):
-        own_in(k).start()
+    def h_in(p):
+        kind, k = order[p]
+        return pltpu.make_async_copy(attn_ref.at[owner_of[kind], :, pl.ds(k * LN, LN)], hloc(kind, None, k, ALL), hsem.at[p // 4])
+
+    for p in range(NP):
+        h_in(p).start()
     xin = pltpu.make_async_copy(x_ref.at[:, pl.ds(pl.multiple_of(t * dt, LN), dt)], xm, lsem.at[1])
     xin.start()
-    for k in range(KP):
-        own_in(k).wait()
-    for k in range(KP):
-        gh.send(k)
 
     per = F // dt
     SR = wo_ref.shape[4]
@@ -271,7 +441,6 @@
         k = jnp.where(own, p, jnp.where(pair, (p - KP) // 2, p - 3 * KP))
         who = jnp.where(own, t, jnp.where(pair, jnp.where(lax.rem(p - KP, 2) == 0, up, dn), op))
         row = pl.multiple_of(who * dt + k * LN, LN)
-        src = wg_ref if False else None
         return row
 
     def w_start(i, slot):
@@ -305,9 +474,8 @@
         for jj in range(NG):
             @pl.when(j == jj)
             def _():
-                wait_group(gh, jj)
-                pltpu.make_async_copy(wo_ref.at[0, 0, layer, 0], ring.at[0, pl.ds(0, SR), pl.ds(0, dt)],
-                                      wosem.at[jj]) if False else None
+                for q in range(4):
+                    h_in(4 * jj + q).wait()
                 for q in range(4):
                     for s in range(NS):
                         wo_copy(4 * jj + q, s).wait()
@@ -321,7 +489,6 @@
     for s in range(min(NSLOT, 2 * NG)):
         if s not in free:
             w_start(jnp.int32(s), s)
-    gh.done()
     xin.wait()
     ss = jnp.zeros((n, LN), jnp.float32)
     for k in range(KP):
@@ -332,6 +499,8 @@
         acc[k] = jnp.zeros(acc.shape[1:], acc.dtype)
     sb = jnp.broadcast_to(jnp.sum(ss, axis=1, keepdims=True), (n, LN))
     st[...] = jnp.swapaxes(sb, 0, 1)[:8]
+
+    pl.semaphore_wait(barrier, 3)
 
     def s_copy(j, dev):
         return rcopy(st, strv.at[j], sts.at[j], strs.at[j], dev)
@@ -519,7 +688,7 @@
             pltpu.VMEM((8, n), f32),
             pltpu.VMEM((3, 8, n), f32),
             D((4, KP)), D((4, KP)), D((6, KP)), D((6, KP)), D((3,)), D((3,)),
-            D((2,)), D((3,)), D((NG,)), D((2,)),
+            D((2,)), D((3,)), D((NG,)), D((2,)), D((NG,)),
         ],
         compiler_params=pltpu.CompilerParams(vmem_limit_bytes=61 * 2 ** 20, collective_id=cid, has_side_effects=True),
         cost_estimate=pl.CostEstimate(flops=2 * n * d * (3 * F + dt), bytes_accessed=2 * d * (3 * F + dt), transcendentals=n * F),
@@ -538,7 +707,6 @@
     def body(x, pos, k_hist, v_hist, wq, wk, wv, wo, wg, wu, wd, g1, g2):
         n, d = x.shape
         layers, hc, kvl, dh = k_hist.shape
-        hql = wq.shape[-1] // dh
         dt = d // tp
         tt, ss = lax.axis_index('tp'), lax.axis_index('sp')
         kp = dt // LN
@@ -553,23 +721,20 @@
         for j in range(1, tp):
             got = lax.ppermute(wcols(lax.rem(tt + j, tp)), 'tp', [(i, (i + j) % tp) for i in range(tp)])
             parts = lax.dynamic_update_index_in_dim(parts, got, lax.rem(tt + tp - j, tp), 0)
-        kv = jnp.stack([k_hist[:, :, 0], v_hist[:, :, 0]], axis=1).reshape(2 * layers, hc, dh)
-        hist = lax.all_gather(kv, 'sp', axis=0)
+        wo_g = lax.all_gather(parts, 'sp', axis=0)
+        kh, vh = k_hist.reshape(layers, hc, dh), v_hist.reshape(layers, hc, dh)
+        half = dh // 2
+        inv = ROPE_THETA ** (-(jnp.arange(half, dtype=jnp.float32) * (2.0 / dh)))
+        ang = pos.astype(jnp.float32)[:, None] * inv
+        cos, sin = jnp.cos(ang), jnp.sin(ang)
+        cos = jnp.concatenate([cos, cos], axis=1)
+        sin = jnp.concatenate([-sin, sin], axis=1)
         ks, vs = [], []
-        wo_g = None
-
         for l in range(layers):
-            h = rmsnorm(x, g1[l])
-            k = rope(mm(h, wk[l]).astype(jnp.bfloat16).reshape(n, kvl, dh), pos)
-            v = mm(h, wv[l]).astype(jnp.bfloat16).reshape(n, kvl, dh)
-            ks.append(k)
-            vs.append(v)
-            new = lax.all_gather(jnp.stack([k[:, 0], v[:, 0]]), 'sp', axis=0)
-            if wo_g is None:
-                wo_g = lax.all_gather(parts, 'sp', axis=0)
-            q = rope(mm(h, wq[l]).astype(jnp.bfloat16).reshape(n, hql, dh), pos)
-            attn = attention(sp, l, q.reshape(n, hql * dh), hist, new)
-            x = mlp(tp, l, attn, x, wo_g, g2[l:l + 1], wg, wu, wd, l)
+            attn, k, v = attention(tp, sp, l, x, cos, sin, kh, vh, wq, wk, wv, g1[l:l + 1], 2 * l)
+            ks.append(k.reshape(n, kvl, dh))
+            vs.append(v.reshape(n, kvl, dh))
+            x = mlp(tp, l, attn, x, wo_g, g2[l:l + 1], wg, wu, wd, 2 * l + 1)
         return x, jnp.stack(ks), jnp.stack(vs)
 
     in_specs = (P(row, None), P(row), kv_spec, kv_spec, col, col, col, rowsplit, col, col, rowsplit, P(), P())

time: 648 us -> 549 us (0.85)
  the two profiles are of different devices: /device:TPU:103 before, /device:TPU:100 now
where the time goes in v3:
time: 549 us
  Pallas kernels  497 us (91%)
  waiting for transfers between devices  15.8 us (3%)
  between operations  14.3 us (3%)
  local copies, waits for them, and re-layouts  10.9 us (2%)
  starting transfers between devices  6.97 us (1%)
    pallas_call x2, Pallas kernels, mlp(): pl.pallas_call(functools.partial(mlp_kernel, T, layer), out_shape=jax.Sha...  298 us
    pallas_call x2, Pallas kernels, attention(): pl.pallas_call(functools.partial(attn_kernel, T, SP, layer), out_shape=[j...  199 us
    ppermute x3, waiting for transfers between devices, body(): lax.ppermute(wcols(lax.rem(tt + j, tp)), 'tp', [(i, (i + j) % tp) for i i...  15.7 us
  transfers between devices with their start and end apart: 4, of which 2 were waited for; matrix products, arithmetic and copies ran while one was open for 1% of the time, Pallas kernels for 20%

profile of v3, /device:TPU:100, one launch (start us, length us, event | category | flops | bytes accessed | tf_op | source)
XLA Modules:
  0.0 548.6 jit_solution(17729424030464606623)
XLA Ops:
  7.2 0.1 all-gather.2.cloned.1.call-start
  7.3 2.9 dynamic-slice_bitcast_fusion
  10.1 2.1 collective-permute-start
  12.3 4.0 collective-permute-start.1
  16.3 0.8 collective-permute-start.2
  17.0 0.1 all_gather.14
  17.2 1.2 bitcast_dynamic-update-slice_fusion
  18.4 0.0 copy-start.7
  18.4 5.7 %collective-permute-done = bf16[2,7,16,896]{3,2,1,0:T(8,128)(2,1)S(1)} collective-permute-done((bf16[2,7,16,896]{3,2,1,0:T(8,128)(2,1)}, bf16[2,7,16,896]{3,2,1,0:T(8,128)(2,1)S(1)}, u32[]{:S(2)}, u32[]{:S(2)}) %collective-permute-start) | collective-permute-done | bytes 401440 | tf_op jit(solution)/shard_map/ppermute | solution.py:722
  24.2 10.0 %collective-permute-done.1 = bf16[2,7,16,896]{3,2,1,0:T(8,128)(2,1)S(1)} collective-permute-done((bf16[2,7,16,896]{3,2,1,0:T(8,128)(2,1)}, bf16[2,7,16,896]{3,2,1,0:T(8,128)(2,1)S(1)}, u32[]{:S(2)}, u32[]{:S(2)}) %collective-permute-start.1) | collective-permute-done | bytes 401440 | tf_op jit(solution)/shard_map/ppermute | solution.py:722
  34.3 1.1 copy-done
  35.4 0.1 all-gather.2.cloned.1.call-update
  35.5 1.0 fusion
  36.5 1.0 pad_maximum_fusion
  37.5 0.6 fusion.2
  38.2 0.6 fusion.1
  38.8 108.4 %attention.2 = (bf16[4,512,896]{2,1,0:T(8,128)(2,1)}, bf16[512,128]{1,0:T(8,128)(2,1)}, bf16[512,128]{1,0:T(8,128)(2,1)}) custom-call(bf16[512,3584]{1,0:T(8,128)(2,1)} %x_ref.3, f32[512,128]{1,0:T(8,128)} %get-tuple-element.25.cos_ref, f32[512,128]{1,0:T(8,128)} %get-tuple-element.26.sin_ref, bf16[2,1024,128]{2,1,0:T(8,128)(2,1)} %bitcast.35, ...), custom_call_target="tpu_custom_call" | custom-call | flops 23018340352 | bytes 5242880 | tf_op jit(solution)/shard_map/attention/pallas_call | solution.py:304
  147.2 0.0 all-gather.2.cloned.1.call-done.wo_ref
  147.3 149.3 %mlp.2.x_ref = bf16[512,3584]{1,0:T(8,128)(2,1)} custom-call(bf16[4,512,896]{2,1,0:T(8,128)(2,1)} %get-tuple-element.9.attn_ref, bf16[512,3584]{1,0:T(8,128)(2,1)} %x_ref.3, bf16[8,4,2,7,16,896]{5,4,3,2,1,0:T(8,128)(2,1)} %all-gather.2.cloned.1.call-done.wo_ref, bf16[1,3584]{1,0:T(2,128)(2,1)} %get-tuple-element.19.g_ref, bf16[2,3584,4736]{2,1,0:T(8,128)(2,1)} %wg_ref.3, ...), custom_call_target="tpu_custom_call" | custom-call | flops 55431921664 | bytes 108265472 | tf_op jit(solution)/shard_map/mlp/pallas_call | solution.py:671
  296.5 90.5 %attention.3 = (bf16[4,512,896]{2,1,0:T(8,128)(2,1)}, bf16[512,128]{1,0:T(8,128)(2,1)}, bf16[512,128]{1,0:T(8,128)(2,1)}) custom-call(bf16[512,3584]{1,0:T(8,128)(2,1)} %mlp.2.x_ref, f32[512,128]{1,0:T(8,128)} %get-tuple-element.25.cos_ref, f32[512,128]{1,0:T(8,128)} %get-tuple-element.26.sin_ref, bf16[2,1024,128]{2,1,0:T(8,128)(2,1)} %bitcast.36, ...), custom_call_target="tpu_custom_call" | custom-call | flops 23018340352 | bytes 5242880 | tf_op jit(solution)/shard_map/attention/pallas_call | solution.py:304
  387.1 149.0 %mlp.3 = bf16[512,3584]{1,0:T(8,128)(2,1)} custom-call(bf16[4,512,896]{2,1,0:T(8,128)(2,1)} %get-tuple-element.10.attn_ref, bf16[512,3584]{1,0:T(8,128)(2,1)} %mlp.2.x_ref, bf16[8,4,2,7,16,896]{5,4,3,2,1,0:T(8,128)(2,1)} %all-gather.2.cloned.1.call-done.wo_ref, bf16[1,3584]{1,0:T(2,128)(2,1)} %get-tuple-element.18.g_ref, bf16[2,3584,4736]{2,1,0:T(8,128)(2,1)} %wg_ref.3, ...), custom_call_target="tpu_custom_call" | custom-call | flops 55431921664 | bytes 108265472 | tf_op jit(solution)/shard_map/mlp/pallas_call | solution.py:671
  536.1 0.7 pad_maximum_fusion.2
  536.9 0.7 pad_maximum_fusion.3
  537.6 4.1 copy.33
  (20 shorter events, 0.2 us)
Async XLA Ops:
  7.2 140.1 %all-gather.2.cloned.1.call-start = ((), (), s32[]{:S(2)}) async-start(), calls=%async_computation | async-start | bytes 14450688 | tf_op jit(solution)/shard_map/all_gather | solution.py:724
  10.1 14.0 %collective-permute-start = (bf16[2,7,16,896]{3,2,1,0:T(8,128)(2,1)}, bf16[2,7,16,896]{3,2,1,0:T(8,128)(2,1)S(1)}, u32[]{:S(2)}, u32[]{:S(2)}) collective-permute-start(bf16[2,7,16,896]{3,2,1,0:T(8,128)(2,1)} %get-tuple-element.17), channel_id=1, source_target_pairs={{0,8},{8,16},{16,24},{24,0},{1,9},{9,17},{17,25},{25,1},{2,10},{10... | collective-permute-start | bytes 1204232 | tf_op jit(solution)/shard_map/ppermute | solution.py:722
  12.3 21.9 %collective-permute-start.1 = (bf16[2,7,16,896]{3,2,1,0:T(8,128)(2,1)}, bf16[2,7,16,896]{3,2,1,0:T(8,128)(2,1)S(1)}, u32[]{:S(2)}, u32[]{:S(2)}) collective-permute-start(bf16[2,7,16,896]{3,2,1,0:T(8,128)(2,1)} %get-tuple-element.16), channel_id=1, source_target_pairs={{0,16},{8,24},{16,0},{24,8},{1,17},{9,25},{17,1},{25,9},{2,18},{10... | collective-permute-start | bytes 1204232 | tf_op jit(solution)/shard_map/ppermute | solution.py:722
  16.3 17.9 %collective-permute-start.2 = (bf16[2,7,16,896]{3,2,1,0:T(8,128)(2,1)S(1)}, bf16[2,7,16,896]{3,2,1,0:T(8,128)(2,1)S(1)}, u32[]{:S(2)}, u32[]{:S(2)}) collective-permute-start(bf16[2,7,16,896]{3,2,1,0:T(8,128)(2,1)S(1)} %get-tuple-element.15), channel_id=1, source_target_pairs={{0,24},{8,0},{16,8},{24,16},{1,25},{9,1},{17,9},{25,17},{2,26},{10... | collective-permute-start | bytes 1204232 | tf_op jit(solution)/shard_map/ppermute | solution.py:722
  18.4 17.1 %copy-start.7 = (s32[512]{0:T(512)S(1)}, s32[512]{0:T(512)}, u32[]{:S(2)}) copy-start(s32[512]{0:T(512)} %param.14) | copy-start | bytes 6148
  34.3 1.2 copy-start
  34.3 3.2 copy-start.5
  34.3 3.9 copy-start.6
  387.1 149.1 %copy-start.2 = (bf16[512,128]{1,0:T(8,128)(2,1)S(1)}, bf16[512,128]{1,0:T(8,128)(2,1)}, u32[]{:S(2)}) copy-start(bf16[512,128]{1,0:T(8,128)(2,1)} %get-tuple-element.11) | copy-start | bytes 393220
  387.1 149.1 %copy-start.4 = (bf16[512,128]{1,0:T(8,128)(2,1)S(1)}, bf16[512,128]{1,0:T(8,128)(2,1)}, u32[]{:S(2)}) copy-start(bf16[512,128]{1,0:T(8,128)(2,1)} %get-tuple-element.12) | copy-start | bytes 393220
  387.1 149.8 %copy-start.1 = (bf16[512,128]{1,0:T(8,128)(2,1)S(1)}, bf16[512,128]{1,0:T(8,128)(2,1)}, u32[]{:S(2)}) copy-start(bf16[512,128]{1,0:T(8,128)(2,1)} %get-tuple-element.13) | copy-start | bytes 393220
  387.1 149.8 %copy-start.3 = (bf16[512,128]{1,0:T(8,128)(2,1)S(1)}, bf16[512,128]{1,0:T(8,128)(2,1)}, u32[]{:S(2)}) copy-start(bf16[512,128]{1,0:T(8,128)(2,1)} %get-tuple-element.14) | copy-start | bytes 393220
Sparse Core Ops, SparseCore 0:
  35.6 86.4 all-gather.1

commit v4 on v3

--- a/solution.py
+++ b/solution.py
@@ -18,10 +18,10 @@
     return jnp.dot(a, b, preferred_element_type=jnp.float32)
 
 
-def attn_kernel(T, SP, layer, x_ref, cos_ref, sin_ref, kh_ref, vh_ref, wq_ref, wk_ref, wv_ref, g_ref,
-                out_ref, ko_ref, vo_ref,
-                xb, wb, kv, qb, m_ref, l_ref, acc_ref, ga,
-                kvs, kvr, gas, gar, lsem, hsem, wsem):
+def attn_kernel(T, SP, layer, x_ref, cos_ref, sin_ref, kh_ref, vh_ref, wq_ref, wk_ref, wv_ref, wo_ref, g_ref, g2_ref,
+                ho_ref, xo_ref, ko_ref, vo_ref,
+                xb, wb, kv, qb, m_ref, l_ref, acc_ref, ga, wob, xm, hb, st, strv,
+                kvs, kvr, gas, gar, wys, wyr, sts, strs, lsem, hsem, wsem):
     n, d = xb.shape
     w = qb.shape[1]
     dh = kv.shape[3]
@@ -29,8 +29,9 @@
     X = SP // 2
     C = kv.shape[2]
     hc = C // 2
-    R = min(128, n)
-    nt = n // R
+    dt = w
+    nt = 4
+    R = n // nt
     scale = dh ** -0.5 * LOG2E
     me = lax.axis_index("sp")
     t = lax.axis_index("tp")
@@ -38,10 +39,10 @@
     xx = me // 2
     lx, rx, ox = lax.rem(xx + X - 1, X), lax.rem(xx + 1, X), lax.rem(xx + 2, X)
     left, right, part = lx * 2 + c, rx * 2 + c, xx * 2 + 1 - c
-    up, dn = lax.rem(t + 1, T), lax.rem(t + T - 1, T)
+    up, dn, far = lax.rem(t + 1, T), lax.rem(t + T - 1, T), lax.rem(t + 2, T)
 
     barrier = pltpu.get_barrier_semaphore()
-    for dev in ({"sp": left}, {"sp": right}, {"sp": part}, {"tp": up}, {"tp": dn}):
+    for dev in ({"sp": left}, {"sp": right}, {"sp": part}, {"tp": up}, {"tp": dn}, {"tp": far}):
         pl.semaphore_signal(barrier, inc=1, device_id=dev, device_id_type=MESH)
 
     def hist_in(j):
@@ -57,7 +58,28 @@
     for cp in win:
         cp.start()
 
+    def wo_cols(dev):
+        return wo_ref.at[layer, :, me, :, pl.ds(pl.multiple_of(dev * dt, LN), dt)]
+
+    wo_own = pltpu.make_async_copy(wo_cols(t), wob.at[t, :, me], wsem.at[2])
+    wo_own.start()
+    xcol = pltpu.make_async_copy(x_ref.at[:, pl.ds(pl.multiple_of(t * dt, LN), dt)], xm, lsem.at[1])
+    xcol.start()
+    peers = ((0, up, dn), (1, dn, up), (2, far, far))
+
+    def wo_tx(j, dev):
+        return pltpu.make_async_remote_copy(src_ref=wo_cols(dev), dst_ref=wob.at[t, :, me], send_sem=wys.at[j],
+                                            recv_sem=wyr.at[j], device_id={"tp": dev}, device_id_type=MESH)
+
+    def wo_rx(j, src):
+        pltpu.make_async_remote_copy(src_ref=wob.at[src, :, me], dst_ref=wob.at[src, :, me], send_sem=wys.at[j],
+                                     recv_sem=wyr.at[j], device_id={"tp": src}, device_id_type=MESH).wait_recv()
+
     def region(kind, chip, core, half):
+        if kind == 2:
+            if half is None:
+                return wob.at[:, :, chip * 2 + core]
+            return wob.at[pl.ds(half * (T // 2), T // 2), :, chip * 2 + core]
         if kind == 0:
             blk, base, ln = chip, core * hc, hc
         else:
@@ -102,10 +124,12 @@
         rx_wait(kind, 4)
         tx(kind, 8).start()
 
-    pl.semaphore_wait(barrier, 5)
+    pl.semaphore_wait(barrier, 6)
     for j in range(2):
         hist_in(j).wait()
     send_own(0)
+    for j, dev, _ in peers:
+        wo_tx(j, dev).start()
 
     xin.wait()
     g = g_ref[...].astype(jnp.float32)
@@ -206,7 +230,6 @@
 
     def g_wait(i, tile):
         base = pl.multiple_of(tile * R, R)
-        far = lax.rem(t + 2, T)
         owner, off, ln = ((dn, 0, R), (up, 0, R), (far, 0, hR), (far, hR, hR))[i]
         ref = ga.at[owner, pl.ds(pl.multiple_of(base + off, hR), ln), :]
         pltpu.make_async_remote_copy(src_ref=ref, dst_ref=ref, send_sem=gas.at[i, tile], recv_sem=gar.at[i, tile],
@@ -224,13 +247,76 @@
             l = jnp.sum(l_ref[h, rows, :], axis=1, keepdims=True)
             ga[t, rows, h * dh:(h + 1) * dh] = (acc_ref[h, rows, :] / l).astype(jnp.bfloat16)
 
+    def tile_rows(tile):
+        return pl.ds(pl.multiple_of(tile * R, R), R)
+
+    def s_copy(j, dev, tile):
+        return pltpu.make_async_remote_copy(src_ref=st.at[tile], dst_ref=strv.at[j, tile], send_sem=sts.at[j, tile],
+                                            recv_sem=strs.at[j, tile], device_id={"tp": dev}, device_id_type=MESH)
+
+    def wo_tile(tile):
+        g_wait(2, tile)
+        g_wait(3, tile)
+        rows = tile_rows(tile)
+        a = jnp.concatenate([ga[j, rows, :] for j in range(T)], axis=1)
+        y = mm(a, wob[...].reshape(d, dt))
+        v = xm[rows, :] + y.astype(jnp.bfloat16)
+        xm[rows, :] = v
+        vf = v.astype(jnp.float32)
+        sb = jnp.broadcast_to(jnp.sum(vf * vf, axis=1, keepdims=True), (R, LN))
+        st[tile] = jnp.swapaxes(sb, 0, 1)[:8]
+        for j, dev, _ in peers:
+            s_copy(j, dev, tile).start()
+
+    def h_tile(tile):
+        rows = tile_rows(tile)
+        for j, dev, _ in peers:
+            s_copy(j, dev, tile).wait_recv()
+        tot = st[tile] + strv[0, tile] + strv[1, tile] + strv[2, tile]
+        r8 = lax.rsqrt(tot / d + EPS)
+        rb = jnp.swapaxes(jnp.concatenate([r8] * (LN // 8), axis=0), 0, 1)
+        for k in range(dt // LN):
+            cols = slice(k * LN, (k + 1) * LN)
+            gk = g2_ref[0:1, pl.ds(pl.multiple_of(t * dt + k * LN, LN), LN)].astype(jnp.float32)
+            hb[rows, cols] = (xm[rows, cols].astype(jnp.float32) * rb * gk).astype(jnp.bfloat16)
+
     rx_wait(0, 2)
     first = 3 * nt
     per = 1 + xx // 2
-    pts = [2, nt, 2 * nt - 2, 2 * nt] if nt >= 4 else [0, 1, 2, 3]
+    total = first + nt * per
+
+    def near(kind):
+        pass_near(kind)
+        if kind == 1:
+            wo_own.wait()
+            for j, _, src in peers:
+                wo_rx(j, src)
+            send_own(2)
+
+    points = ((2, near, 0), (nt, near, 1), (2 * nt - 1, pass_far, 0), (2 * nt, pass_far, 1), (first + 2, near, 2))
+
+    def post(stage):
+        @pl.when(jnp.logical_and(stage >= 1, stage <= nt))
+        def _():
+            g_pass(stage - 1)
+
+        @pl.when(stage == 2)
+        def _():
+            pass_far(2)
+            for gid in (2, 5, 6, 7, 8):
+                rx_wait(2, gid)
+            xcol.wait()
+
+        @pl.when(jnp.logical_and(stage >= 2, stage <= nt + 1))
+        def _():
+            wo_tile(stage - 2)
+
+        @pl.when(stage >= 3)
+        def _():
+            h_tile(stage - 3)
 
     def step(i, carry):
-        for at, fn, kind in zip(pts, (pass_near, pass_near, pass_far, pass_far), (0, 1, 0, 1)):
+        for at, fn, kind in points:
             @pl.when(i == at)
             def _():
                 fn(kind)
@@ -253,13 +339,14 @@
         tile = jnp.where(late, i2 // per, lax.rem(i, nt))
         early = jnp.where(i < nt, xx, jnp.where(i < 2 * nt, lx, rx))
         blk = jnp.where(late, jnp.where(m == 0, ox, X + m - 1), early)
-        unit(tile, blk, None)
-
-        @pl.when(jnp.logical_and(late, jnp.logical_and(m == 0, tile >= 2)))
-        def _():
-            g_pass(tile - 2)
-
-        @pl.when(jnp.logical_and(late, m == per - 1))
+        live = i < total
+        last = jnp.logical_and(jnp.logical_and(late, live), m == per - 1)
+
+        @pl.when(live)
+        def _():
+            unit(tile, blk, None)
+
+        @pl.when(last)
         def _():
             off = lax.rem(xx, 2) * (2 * n) + c * n + tile * R
             row = lax.broadcasted_iota(jnp.int32, (R, C), 0) + off
@@ -267,35 +354,41 @@
             finish(tile)
             gx(0, tile).start()
             gx(1, tile).start()
+
+        @pl.when(jnp.logical_or(last, jnp.logical_not(live)))
+        def _():
+            post(jnp.where(live, tile, nt + i - total))
         return carry
 
-    lax.fori_loop(0, first + nt * per, step, 0)
-    for tile in range(max(nt - 2, 0), nt):
-        g_pass(tile)
-    for tile in range(nt):
-        g_wait(2, tile)
-        g_wait(3, tile)
-    o = pltpu.make_async_copy(ga, out_ref, lsem.at[0])
-    o.start()
+    lax.fori_loop(0, total + 3, step, 0)
+    o1 = pltpu.make_async_copy(hb, ho_ref, lsem.at[0])
+    o2 = pltpu.make_async_copy(xm, xo_ref, lsem.at[1])
+    o1.start()
+    o2.start()
     for tile in range(nt):
         for i in range(4):
             gx(i, tile).wait_send()
-    for kind in range(2):
+        for j, dev, _ in peers:
+            s_copy(j, dev, tile).wait_send()
+    for j, dev, _ in peers:
+        wo_tx(j, dev).wait_send()
+    for kind in range(3):
         for i in range(9):
             tx(kind, i).wait_send()
     for j in range(2):
         kv_out(j).wait()
-    o.wait()
-
-
-def attention(T, SP, layer, x, cos, sin, kh, vh, wq, wk, wv, g, cid):
+    o1.wait()
+    o2.wait()
+
+
+def attention(T, SP, layer, x, cos, sin, kh, vh, wq, wk, wv, wo, g, g2, cid):
     n, d = x.shape
     w = wq.shape[2]
     hc, dh = kh.shape[1], kh.shape[2]
     heads = w // dh
     X = SP // 2
-    assert 2 * hc == 4 * n and wk.shape[2] == dh
-    R = min(128, n)
+    assert 2 * hc == 4 * n and wk.shape[2] == dh and w * T == d
+    R = n // 4
     f32, bf = jnp.float32, jnp.bfloat16
     hbm = pl.BlockSpec(memory_space=pltpu.HBM)
     vm = pl.BlockSpec(memory_space=pltpu.VMEM)
@@ -303,9 +396,10 @@
     keys = SP * (hc + n // 2)
     return pl.pallas_call(
         functools.partial(attn_kernel, T, SP, layer),
-        out_shape=[jax.ShapeDtypeStruct((T, n, w), bf), jax.ShapeDtypeStruct((n, dh), bf), jax.ShapeDtypeStruct((n, dh), bf)],
-        in_specs=[hbm, vm, vm, hbm, hbm, hbm, hbm, hbm, vm],
-        out_specs=[hbm, hbm, hbm],
+        out_shape=[jax.ShapeDtypeStruct((n, w), bf), jax.ShapeDtypeStruct((n, w), bf),
+                   jax.ShapeDtypeStruct((n, dh), bf), jax.ShapeDtypeStruct((n, dh), bf)],
+        in_specs=[hbm, vm, vm, hbm, hbm, hbm, hbm, hbm, hbm, vm, vm],
+        out_specs=[hbm, hbm, hbm, hbm],
         scratch_shapes=[
             pltpu.VMEM((n, d), bf),
             pltpu.VMEM((d, w + 2 * dh), bf),
@@ -315,18 +409,23 @@
             pltpu.VMEM((heads, n, LN), f32),
             pltpu.VMEM((heads, n, dh), f32),
             pltpu.VMEM((T, n, w), bf),
-            D((2, 9)), D((2, 9)), D((4, n // R)), D((4, n // R)), D((2,)), D, D((2,)),
+            pltpu.VMEM((T, w // LN, SP, LN // SP, w), bf),
+            pltpu.VMEM((n, w), bf),
+            pltpu.VMEM((n, w), bf),
+            pltpu.VMEM((4, 8, R), f32),
+            pltpu.VMEM((3, 4, 8, R), f32),
+            D((3, 9)), D((3, 9)), D((4, 4)), D((4, 4)), D((3,)), D((3,)), D((3, 4)), D((3, 4)), D((2,)), D, D((3,)),
         ],
         compiler_params=pltpu.CompilerParams(vmem_limit_bytes=61 * 2 ** 20, collective_id=cid, has_side_effects=True),
         cost_estimate=pl.CostEstimate(flops=4 * n * w * keys + 2 * n * d * (w + 2 * dh), bytes_accessed=4 * keys * dh,
                                       transcendentals=n * heads * keys),
         name="attention",
-    )(x, cos, sin, kh, vh, wq, wk, wv, g)
-
-
-def mlp_kernel(T, layer, attn_ref, x_ref, wo_ref, g_ref, wg_ref, wu_ref, wd_ref, out_ref,
-               acc, ring, H, U, wdb, RA, RB, RD, RU, XF, xm, st, strv,
-               ags, agr, rss, rsr, sts, strs, lsem, wsem, wosem, dsem, hsem):
+    )(x, cos, sin, kh, vh, wq, wk, wv, wo.reshape(wo.shape[0], w // LN, SP, LN // SP, d), g, g2)
+
+
+def mlp_kernel(T, layer, h_ref, x_ref, wg_ref, wu_ref, wd_ref, out_ref,
+               acc, ring, H, U, wdb, RA, RB, RD, RU, XF, xm,
+               ags, agr, rss, rsr, lsem, wsem, dsem):
     n, d = XF.shape
     dt = d // T
     KP = dt // LN
@@ -410,29 +509,13 @@
         for kind, k in order[4 * j:4 * j + 4]:
             gather.wait(kind, k)
 
-    def h_in(p):
-        kind, k = order[p]
-        return pltpu.make_async_copy(attn_ref.at[owner_of[kind], :, pl.ds(k * LN, LN)], hloc(kind, None, k, ALL), hsem.at[p // 4])
-
-    for p in range(NP):
-        h_in(p).start()
-    xin = pltpu.make_async_copy(x_ref.at[:, pl.ds(pl.multiple_of(t * dt, LN), dt)], xm, lsem.at[1])
+    def h_in(k):
+        return pltpu.make_async_copy(h_ref.at[:, pl.ds(k * LN, LN)], hloc('own', t, k, ALL), lsem.at[0])
+
+    for k in range(KP):
+        h_in(k).start()
+    xin = pltpu.make_async_copy(x_ref, xm, lsem.at[1])
     xin.start()
-
-    per = F // dt
-    SR = wo_ref.shape[4]
-    NS = wo_ref.shape[0]
-
-    def wo_copy(p, s):
-        kind, k = order[p]
-        j = p // 4
-        return pltpu.make_async_copy(
-            wo_ref.at[s, owner_of[kind], layer, k],
-            ring.at[j // per, pl.ds((p % 4) * LN + s * SR, SR), pl.ds((j % per) * dt, dt)], wosem.at[j])
-
-    for p in range(NP):
-        for s in range(NS):
-            wo_copy(p, s).start()
 
     def w_copy(i, q, slot):
         p = (i // 2) * 4 + q
@@ -460,67 +543,19 @@
         pltpu.make_async_copy(wg_ref.at[layer, pl.ds(0, 4 * LN), :], ring.at[slot], wsem.at[slot]).wait()
 
     NSLOT = ring.shape[0]
-    free = list(range((NG + per - 1) // per, NSLOT))
-    for s in free:
+    for s in range(NSLOT):
         w_start(jnp.int32(s), s)
+    for k in range(KP):
+        h_in(k).wait()
+    pl.semaphore_wait(barrier, 3)
+    for k in range(KP):
+        gh.send(k)
 
     def zero(j, c):
         acc[j] = jnp.zeros(acc.shape[1:], acc.dtype)
         return c
 
     lax.fori_loop(0, 2 * FP, zero, 0)
-
-    def wo_step(j, c):
-        for jj in range(NG):
-            @pl.when(j == jj)
-            def _():
-                for q in range(4):
-                    h_in(4 * jj + q).wait()
-                for q in range(4):
-                    for s in range(NS):
-                        wo_copy(4 * jj + q, s).wait()
-        w = ring[j // per, :, pl.ds(pl.multiple_of(lax.rem(j, per) * dt, LN), dt)]
-        r = mm(H[j], w)
-        for k in range(KP):
-            acc[k] += r[:, k * LN:(k + 1) * LN]
-        return c
-
-    lax.fori_loop(0, NG, wo_step, 0)
-    for s in range(min(NSLOT, 2 * NG)):
-        if s not in free:
-            w_start(jnp.int32(s), s)
-    xin.wait()
-    ss = jnp.zeros((n, LN), jnp.float32)
-    for k in range(KP):
-        v = xm[:, k * LN:(k + 1) * LN] + acc[k].astype(jnp.bfloat16)
-        xm[:, k * LN:(k + 1) * LN] = v
-        vf = v.astype(jnp.float32)
-        ss = ss + vf * vf
-        acc[k] = jnp.zeros(acc.shape[1:], acc.dtype)
-    sb = jnp.broadcast_to(jnp.sum(ss, axis=1, keepdims=True), (n, LN))
-    st[...] = jnp.swapaxes(sb, 0, 1)[:8]
-
-    pl.semaphore_wait(barrier, 3)
-
-    def s_copy(j, dev):
-        return rcopy(st, strv.at[j], sts.at[j], strs.at[j], dev)
-
-    peers = ((0, up), (1, dn), (2, op))
-    for j, dev in peers:
-        s_copy(j, dev).start()
-    for j, dev in peers:
-        s_copy(j, dev).wait_recv()
-    tot = st[...] + strv[0] + strv[1] + strv[2]
-    r8 = lax.rsqrt(tot / d + EPS)
-    rb = jnp.swapaxes(jnp.concatenate([r8] * (LN // 8), axis=0), 0, 1)
-    for k in range(KP):
-        gk = g_ref[0, pl.ds(pl.multiple_of(t * dt + k * LN, LN), LN)].astype(jnp.float32)
-        hv = (xm[:, k * LN:(k + 1) * LN].astype(jnp.float32) * rb * gk[None, :]).astype(jnp.bfloat16)
-        H[k // 4, :, (k % 4) * LN:(k % 4 + 1) * LN] = hv
-    for k in range(KP):
-        gh.send(k)
-    for j, dev in peers:
-        s_copy(j, dev).wait_send()
 
     def gu_step(i, c):
         j = i // 2
@@ -634,6 +669,7 @@
 
     lax.fori_loop(0, KP, add, 0)
 
+    xin.wait()
     for k in range(KP):
         c_upB(k).wait_recv()
         c_dnA(k).wait_recv()
@@ -657,10 +693,10 @@
     o.wait()
 
 
-def mlp(T, layer, attn, x, wo_g, g, wg, wu, wd, cid):
-    n, d = x.shape
+def mlp(T, layer, h, x, wg, wu, wd, cid):
+    n, dt = x.shape
     F = wg.shape[2]
-    dt = d // T
+    d = dt * T
     KP = dt // LN
     FP = F // LN
     hf = n // 2
@@ -671,7 +707,7 @@
     return pl.pallas_call(
         functools.partial(mlp_kernel, T, layer),
         out_shape=jax.ShapeDtypeStruct((n, d), bf),
-        in_specs=[anyspec, anyspec, anyspec, pl.BlockSpec(memory_space=pltpu.VMEM), anyspec, anyspec, anyspec],
+        in_specs=[anyspec] * 5,
         out_specs=anyspec,
         scratch_shapes=[
             pltpu.VMEM((2 * FP, n, LN), f32),
@@ -685,15 +721,12 @@
             pltpu.VMEM((KP, n, LN), f32),
             pltpu.VMEM((n, d), bf),
             pltpu.VMEM((n, dt), bf),
-            pltpu.VMEM((8, n), f32),
-            pltpu.VMEM((3, 8, n), f32),
-            D((4, KP)), D((4, KP)), D((6, KP)), D((6, KP)), D((3,)), D((3,)),
-            D((2,)), D((3,)), D((NG,)), D((2,)), D((NG,)),
+            D((4, KP)), D((4, KP)), D((6, KP)), D((6, KP)), D((2,)), D((3,)), D((2,)),
         ],
         compiler_params=pltpu.CompilerParams(vmem_limit_bytes=61 * 2 ** 20, collective_id=cid, has_side_effects=True),
-        cost_estimate=pl.CostEstimate(flops=2 * n * d * (3 * F + dt), bytes_accessed=2 * d * (3 * F + dt), transcendentals=n * F),
+        cost_estimate=pl.CostEstimate(flops=6 * n * d * F, bytes_accessed=6 * d * F, transcendentals=n * F),
         name="mlp",
-    )(attn, x, wo_g, g, wg, wu, wd)
+    )(h, x, wg, wu, wd)
 
 
 def solution(mesh):
@@ -707,21 +740,6 @@
     def body(x, pos, k_hist, v_hist, wq, wk, wv, wo, wg, wu, wd, g1, g2):
         n, d = x.shape
         layers, hc, kvl, dh = k_hist.shape
-        dt = d // tp
-        tt, ss = lax.axis_index('tp'), lax.axis_index('sp')
-        kp = dt // LN
-        sr = LN // sp
-        wr = lax.dynamic_index_in_dim(wo.reshape(layers, kp, sp, sr, d), ss, axis=2, keepdims=False)
-
-        def wcols(t):
-            return lax.dynamic_slice_in_dim(wr, t * dt, dt, axis=3)
-
-        parts = jnp.zeros((tp,) + wcols(0).shape, wo.dtype)
-        parts = lax.dynamic_update_index_in_dim(parts, wcols(tt), tt, 0)
-        for j in range(1, tp):
-            got = lax.ppermute(wcols(lax.rem(tt + j, tp)), 'tp', [(i, (i + j) % tp) for i in range(tp)])
-            parts = lax.dynamic_update_index_in_dim(parts, got, lax.rem(tt + tp - j, tp), 0)
-        wo_g = lax.all_gather(parts, 'sp', axis=0)
         kh, vh = k_hist.reshape(layers, hc, dh), v_hist.reshape(layers, hc, dh)
         half = dh // 2
         inv = ROPE_THETA ** (-(jnp.arange(half, dtype=jnp.float32) * (2.0 / dh)))
@@ -731,10 +749,10 @@
         sin = jnp.concatenate([-sin, sin], axis=1)
         ks, vs = [], []
         for l in range(layers):
-            attn, k, v = attention(tp, sp, l, x, cos, sin, kh, vh, wq, wk, wv, g1[l:l + 1], 2 * l)
+            h, xm, k, v = attention(tp, sp, l, x, cos, sin, kh, vh, wq, wk, wv, wo, g1[l:l + 1], g2[l:l + 1], 2 * l)
             ks.append(k.reshape(n, kvl, dh))
             vs.append(v.reshape(n, kvl, dh))
-            x = mlp(tp, l, attn, x, wo_g, g2[l:l + 1], wg, wu, wd, 2 * l + 1)
+            x = mlp(tp, l, h, xm, wg, wu, wd, 2 * l + 1)
         return x, jnp.stack(ks), jnp.stack(vs)
 
     in_specs = (P(row, None), P(row), kv_spec, kv_spec, col, col, col, rowsplit, col, col, rowsplit, P(), P())

time: 549 us -> 507 us (0.923)
  waiting for transfers between devices: 15.8 us -> 0 us
  between operations: 14.3 us -> 0.7 us
  starting transfers between devices: 6.97 us -> 0 us
    ppermute x3 -> x0, waiting for transfers between devices: 15.7 us -> none  [body(): lax.ppermute(wcols(lax.rem(tt + j, tp)), 'tp', [(i, (i + j) % tp) for i i...]
    pallas_call x2, Pallas kernels: 298 us -> 290 us  [mlp(): pl.pallas_call(functools.partial(mlp_kernel, T, layer), out_shape=jax.Sha...]
    ppermute x3 -> x0, starting transfers between devices: 6.91 us -> none  [body(): lax.ppermute(wcols(lax.rem(tt + j, tp)), 'tp', [(i, (i + j) % tp) for i i...]
    pallas_call x2, Pallas kernels: 199 us -> 205 us  [attention(): pl.pallas_call(functools.partial(attn_kernel, T, SP, layer), out_shape=[j...]
  transfers between devices with their start and end apart: 4 -> 0, of which waited for: 2 -> 0; matrix products, arithmetic and copies ran while one was open for 1% -> 0% of each run, Pallas kernels for 20% -> 0%
where the time goes in v4:
time: 507 us
  Pallas kernels  495 us (98%)
  other arithmetic  5.95 us (1%)
  local copies, waits for them, and re-layouts  5.57 us (1%)
    pallas_call x2, Pallas kernels, mlp(): pl.pallas_call(functools.partial(mlp_kernel, T, layer), out_shape=jax.Sha...  290 us
    pallas_call x2, Pallas kernels, attention(): pl.pallas_call(functools.partial(attn_kernel, T, SP, layer), out_shape=[j...  205 us

profile of v4, /device:TPU:100, one launch (start us, length us, event | category | flops | bytes accessed | tf_op | source)
XLA Modules:
  0.0 507.0 jit_solution(15723895333615793385)
XLA Ops:
  0.6 0.7 convert_element_type.3
  1.3 1.4 fusion.1
  2.8 1.0 fusion
  3.8 1.0 pad_maximum_fusion
  4.8 105.2 %attention.2 = (bf16[512,896]{1,0:T(8,128)(2,1)}, bf16[512,896]{1,0:T(8,128)(2,1)}, bf16[512,128]{1,0:T(8,128)(2,1)}, bf16[512,128]{1,0:T(8,128)(2,1)}) custom-call(bf16[512,3584]{1,0:T(8,128)(2,1)} %x_ref.1, f32[512,128]{1,0:T(8,128)} %get-tuple-element.26.cos_ref, f32[512,128]{1,0:T(8,128)} %get-tuple-element.27.sin_ref, bf16[2,1024,128]{2,1,0:T(8,128)(2,1)} %bitcast.13, ...), custom_call_target="tpu_custom_call" | custom-call | flops 23018340352 | bytes 5242880 | tf_op jit(solution)/shard_map/attention/pallas_call | solution.py:397
  110.0 145.2 %mlp.2.x_ref = bf16[512,3584]{1,0:T(8,128)(2,1)} custom-call(bf16[512,896]{1,0:T(8,128)(2,1)} %get-tuple-element.11.h_ref, bf16[512,896]{1,0:T(8,128)(2,1)} %get-tuple-element.12.x_ref, bf16[2,3584,4736]{2,1,0:T(8,128)(2,1)} %wg_ref.3, bf16[2,3584,4736]{2,1,0:T(8,128)(2,1)} %wu_ref.3, bf16[2,4736,3584]{2,1,0:T(8,128)(2,1)} %wd_ref.3), custom_call_target="tpu_custom_call" | custom-call | flops 52143587328 | bytes 101842944 | tf_op jit(solution)/shard_map/mlp/pallas_call | solution.py:707
  255.2 0.0 copy-start.1
  255.2 0.0 copy-start
  255.2 99.5 %attention.3 = (bf16[512,896]{1,0:T(8,128)(2,1)}, bf16[512,896]{1,0:T(8,128)(2,1)}, bf16[512,128]{1,0:T(8,128)(2,1)}, bf16[512,128]{1,0:T(8,128)(2,1)}) custom-call(bf16[512,3584]{1,0:T(8,128)(2,1)} %mlp.2.x_ref, f32[512,128]{1,0:T(8,128)} %get-tuple-element.26.cos_ref, f32[512,128]{1,0:T(8,128)} %get-tuple-element.27.sin_ref, ...), custom_call_target="tpu_custom_call" | custom-call | flops 23018340352 | bytes 5242880 | tf_op jit(solution)/shard_map/attention/pallas_call | solution.py:397
  354.8 0.0 copy-done.1
  354.8 1.6 pad_maximum_fusion.2
  356.4 0.0 copy-done
  356.4 1.6 pad_maximum_fusion.3
  358.1 144.8 %mlp.3 = bf16[512,3584]{1,0:T(8,128)(2,1)} custom-call(bf16[512,896]{1,0:T(8,128)(2,1)} %get-tuple-element.13.h_ref, bf16[512,896]{1,0:T(8,128)(2,1)} %get-tuple-element.14.x_ref, bf16[2,3584,4736]{2,1,0:T(8,128)(2,1)} %wg_ref.3, bf16[2,3584,4736]{2,1,0:T(8,128)(2,1)} %wu_ref.3, bf16[2,4736,3584]{2,1,0:T(8,128)(2,1)} %wd_ref.3), custom_call_target="tpu_custom_call" | custom-call | flops 52143587328 | bytes 101842944 | tf_op jit(solution)/shard_map/mlp/pallas_call | solution.py:707
  502.8 4.1 copy.17
  (1 shorter events, 0.0 us)
Async XLA Ops:
  255.2 99.6 %copy-start.1 = (bf16[512,128]{1,0:T(8,128)(2,1)S(1)}, bf16[512,128]{1,0:T(8,128)(2,1)}, u32[]{:S(2)}) copy-start(bf16[512,128]{1,0:T(8,128)(2,1)} %get-tuple-element.15) | copy-start | bytes 393220
  255.2 101.2 %copy-start = (bf16[512,128]{1,0:T(8,128)(2,1)S(1)}, bf16[512,128]{1,0:T(8,128)(2,1)}, u32[]{:S(2)}) copy-start(bf16[512,128]{1,0:T(8,128)(2,1)} %get-tuple-element.17) | copy-start | bytes 393220
